TPU v7x, 128 devices: a whole 4x4x4 slice. The times are simulated.
128 devices in a mesh: az: 16 (over z, y), rg: 8 (over x, core).
Axes of the slice: x: 4, y: 4, z: 4, core: 2. Of those that a mesh axis runs over, the one named last changes fastest.
Arguments:
- ref_image: float32 [2048, 6144], P('az', 'rg'), may hold values from 0.2 to 5
- sec_image: float32 [2048, 6144], P('az', 'rg'), may hold values from 0.2 to 5
- off_az: int32 [32], P('az'), may hold values from -15 to 15, as said below
- off_rg: int32 [32], P('az'), may hold values from -15 to 15, as said below
Outputs:
- surfaces: float32 [32, 96, 128, 128], P('az', 'rg')
Inputs may be any that keep to these rules, and one draw needn't show every extreme that they name: off_az is monotone over the chip rows, changes by 0 or 1 between neighbouring chip rows, and runs from one end of its range to the other. off_rg is monotone over the chip rows, changes by 0 or 1 between neighbouring chip rows, and runs from one end of its range to the other.
All inputs are finite; a program needn't handle non-finite values.
Results may differ from a plain program's by a relative error of at most 0.0003.
Values sent between devices are 32-bit elements; how exact they have to be, the bound alone decides.
A program may use at most 64 MiB of HBM per device.

v0:
```python
import math

import jax
import jax.numpy as jnp
from jax import lax
from jax.sharding import PartitionSpec as P

CHIP = 128
SPACE = 64
SEARCH = 192
LAGS = 64


EPSILON = 1e-06
HIGH = lax.Precision.HIGH


def extended(value, sides, width):
    for axis, dim in sides:
        size, length = (lax.axis_size(axis), value.shape[dim])
        up = [(i, (i + 1) % size) for i in range(size - 1)]
        down = [(j, i) for i, j in up]
        last = lax.slice_in_dim(value, length - width, length, axis=dim)
        leading = lax.slice_in_dim(value, 0, width, axis=dim)
        before = lax.ppermute(last, axis, up)
        after = lax.ppermute(leading, axis, down)
        value = jnp.concatenate([before, value, after], axis=dim)
    return value


def box_matrix():
    lag_index = lax.iota(jnp.int32, LAGS)[:, None]
    cell_index = lax.iota(jnp.int32, SEARCH)[None, :]
    return ((cell_index >= lag_index) & (cell_index < lag_index + CHIP)).astype(jnp.float32)


def cubic_matrix():
    out_index = lax.iota(jnp.int32, 2 * LAGS)[:, None]
    sample = lax.iota(jnp.int32, LAGS)[None, :]
    base = out_index // 2

    def pick(where):
        return (jnp.clip(where, 0, LAGS - 1) == sample).astype(jnp.float32)

    even_part = pick(base)
    odd_part = (9.0 * (pick(base) + pick(base + 1)) - (pick(base - 1) + pick(base + 2))) / 16.0
    return jnp.where(out_index % 2 == 1, odd_part, even_part)


def fourier_tables():
    freq = lax.iota(jnp.int32, SEARCH)[:, None]
    cell = lax.iota(jnp.int32, SEARCH)[None, :]
    angle = (freq * cell % SEARCH).astype(jnp.float32) * (2.0 * math.pi / SEARCH)
    return (jnp.cos(angle), jnp.sin(angle))


def cut_chips(band, count):
    blocks = band.reshape(band.shape[0], count + 1, SPACE)
    joined = jnp.concatenate([blocks[:, :-1], blocks[:, 1:]], axis=2)
    return jnp.transpose(joined, (1, 0, 2))


def cut_windows(band, count):
    blocks = band.reshape(band.shape[0], count + 2, SPACE)
    joined = jnp.concatenate([blocks[:, :-2], blocks[:, 1:-1], blocks[:, 2:]], axis=2)
    return jnp.transpose(joined, (1, 0, 2))


def spectrum_of(field, left_cos, left_sin, right_cos, right_sin):
    first_re = jnp.einsum("ua,nab->nub", left_cos, field, precision=HIGH)
    first_im = -jnp.einsum("ua,nab->nub", left_sin, field, precision=HIGH)
    real_part = jnp.einsum("nub,vb->nuv", first_re, right_cos, precision=HIGH) + jnp.einsum(
        "nub,vb->nuv", first_im, right_sin, precision=HIGH
    )
    imag_part = jnp.einsum("nub,vb->nuv", first_im, right_cos, precision=HIGH) - jnp.einsum(
        "nub,vb->nuv", first_re, right_sin, precision=HIGH
    )
    return (real_part, imag_part)


def correlate(centered, windows):
    cosine, sine_table = fourier_tables()
    chip_re, chip_im = spectrum_of(
        centered, cosine[:, :CHIP], sine_table[:, :CHIP], cosine[:, :CHIP], sine_table[:, :CHIP]
    )
    win_re, win_im = spectrum_of(windows, cosine, sine_table, cosine, sine_table)
    prod_re = chip_re * win_re + chip_im * win_im
    prod_im = chip_re * win_im - chip_im * win_re
    back_cos = cosine[:LAGS]
    back_sin = sine_table[:LAGS]
    inner_re = jnp.einsum("pu,nuv->npv", back_cos, prod_re, precision=HIGH) - jnp.einsum(
        "pu,nuv->npv", back_sin, prod_im, precision=HIGH
    )
    inner_im = jnp.einsum("pu,nuv->npv", back_cos, prod_im, precision=HIGH) + jnp.einsum(
        "pu,nuv->npv", back_sin, prod_re, precision=HIGH
    )
    result = jnp.einsum("npv,qv->npq", inner_re, back_cos, precision=HIGH) - jnp.einsum(
        "npv,qv->npq", inner_im, back_sin, precision=HIGH
    )
    return result / float(SEARCH * SEARCH)


def finish(corr, centered, windows):
    box_sum = box_matrix()
    first = jnp.einsum("pr,nrs->nps", box_sum, windows, precision=HIGH)
    first = jnp.einsum("nps,qs->npq", first, box_sum, precision=HIGH)
    second = jnp.einsum("pr,nrs->nps", box_sum, windows * windows, precision=HIGH)
    second = jnp.einsum("nps,qs->npq", second, box_sum, precision=HIGH)
    area = float(CHIP * CHIP)
    var_sum = second - first * first / area
    energy = jnp.sum(centered * centered, axis=(1, 2))
    score = (
        CHIP * (corr / area) / jnp.sqrt(energy[:, None, None] / area * (var_sum / area) + EPSILON)
    )
    oversample = cubic_matrix()
    lifted = jnp.einsum("ap,npq->naq", oversample, score, precision=HIGH)
    return jnp.einsum("naq,bq->nab", lifted, oversample, precision=HIGH)


def body(ref_image, sec_image, off_az, off_rg):
    rows_dev = ref_image.shape[0]
    cols_dev = ref_image.shape[1]
    quarter = CHIP // 4
    half_chip = CHIP // 2
    chip_rows = rows_dev // SPACE
    chip_cols = cols_dev // SPACE
    all_rows = chip_rows * lax.axis_size("az")
    reach = min(half_chip - 1, (all_rows - 1) // 2)
    margin = half_chip + reach
    ref_ext = extended(ref_image, (("az", 0), ("rg", 1)), quarter)
    stacked = sec_image[None]
    widened = extended(extended(stacked, (("rg", 2),), margin), (("az", 1),), margin)
    sec_ext = widened[0]

    def one_row(inputs):
        row_index, shift_az, shift_rg = inputs
        ref_band = lax.dynamic_slice_in_dim(ref_ext, row_index * SPACE, CHIP, 0)
        chips = cut_chips(ref_band, chip_cols)
        sec_rows = lax.dynamic_slice_in_dim(
            sec_ext, row_index * SPACE + shift_az - half_chip + margin, SEARCH, 0
        )
        sec_band = lax.dynamic_slice_in_dim(
            sec_rows, shift_rg - half_chip + margin, chip_cols * SPACE + CHIP, 1
        )
        windows = cut_windows(sec_band, chip_cols)
        centered = chips - jnp.mean(chips, axis=(1, 2), keepdims=True)
        corr = correlate(centered, windows)
        return finish(corr, centered, windows)

    row_list = lax.iota(jnp.int32, chip_rows)
    return lax.map(one_row, (row_list, off_az, off_rg))


def solution(mesh):
    return jax.shard_map(
        body,
        mesh=mesh,
        in_specs=(P("az", "rg"), P("az", "rg"), P("az"), P("az")),
        out_specs=P("az", "rg", None, None),
        check_vma=False,
    )
```

profile of v0, /device:TPU:26, one launch (start us, length us, event | category | flops | bytes accessed | tf_op | source)
XLA Modules:
  0.0 136.5 jit_solution(3348626864240987119)
XLA Ops:
  0.0 1.1 copy.19
  1.2 1.9 %collective-permute-start.4 = (f32[1,128,79]{1,2,0:T(8,128)S(1)}, f32[1,128,79]{1,2,0:T(8,128)S(1)}, u32[]{:S(2)}, u32[]{:S(2)}) collective-permute-start(f32[1,128,79]{1,2,0:T(8,128)S(1)} %get-tuple-element.337), channel_id=1, source_target_pairs={{0,1},{1,2},{2,3},{3,4},{4,5},{5,6},{6,7},{8,9},{9,10},{10,11},{11... | collective-permute-start | bytes 121352 | tf_op jit(solution)/shard_map/ppermute | solution.py:25
  3.1 3.6 %collective-permute-start.5 = (f32[1,128,79]{1,2,0:T(8,128)S(1)}, f32[1,128,79]{1,2,0:T(8,128)S(1)}, u32[]{:S(2)}, u32[]{:S(2)}) collective-permute-start(f32[1,128,79]{1,2,0:T(8,128)S(1)} %get-tuple-element.338), channel_id=1, source_target_pairs={{1,0},{2,1},{3,2},{4,3},{5,4},{6,5},{7,6},{9,8},{10,9},{11,10},{12... | collective-permute-start | bytes 121352 | tf_op jit(solution)/shard_map/ppermute | solution.py:26
  6.8 1.2 copy.16
  8.1 3.5 %collective-permute-start = (f32[32,768]{0,1:T(8,128)S(1)}, f32[32,768]{0,1:T(8,128)S(1)}, u32[]{:S(2)}, u32[]{:S(2)}) collective-permute-start(f32[32,768]{0,1:T(8,128)S(1)} %get-tuple-element.339), channel_id=1, source_target_pairs={{0,8},{8,16},{16,24},{24,32},{32,40},{40,48},{48,56},{56,64},{64,7... | collective-permute-start | bytes 294920 | tf_op jit(solution)/shard_map/ppermute | solution.py:25
  11.6 2.4 %collective-permute-start.1 = (f32[32,768]{0,1:T(8,128)S(1)}, f32[32,768]{0,1:T(8,128)S(1)}, u32[]{:S(2)}, u32[]{:S(2)}) collective-permute-start(f32[32,768]{0,1:T(8,128)S(1)} %get-tuple-element.340), channel_id=1, source_target_pairs={{8,0},{16,8},{24,16},{32,24},{40,32},{48,40},{56,48},{64,56},{72,6... | collective-permute-start | bytes 294920 | tf_op jit(solution)/shard_map/ppermute | solution.py:26
  14.0 1.1 fusion.122
  15.1 5.6 %collective-permute-start.6 = (f32[1,79,926]{1,2,0:T(8,128)}, f32[1,79,926]{1,2,0:T(8,128)S(1)}, u32[]{:S(2)}, u32[]{:S(2)}) collective-permute-start(f32[1,79,926]{1,2,0:T(8,128)} %get-tuple-element.335), channel_id=1, source_target_pairs={{0,8},{8,16},{16,24},{24,32},{32,40},{40,48},{48,56},{56,64},{64,7... | collective-permute-start | bytes 877856 | tf_op jit(solution)/shard_map/ppermute | solution.py:25
  20.7 1.9 %collective-permute-start.7 = (f32[1,79,926]{1,2,0:T(8,128)}, f32[1,79,926]{1,2,0:T(8,128)}, u32[]{:S(2)}, u32[]{:S(2)}) collective-permute-start(f32[1,79,926]{1,2,0:T(8,128)} %get-tuple-element.336), channel_id=1, source_target_pairs={{8,0},{16,8},{24,16},{32,24},{40,32},{48,40},{56,48},{64,56},{72,6... | collective-permute-start | bytes 877856 | tf_op jit(solution)/shard_map/ppermute | solution.py:26
  22.6 3.6 %collective-permute-done.1 = f32[32,768]{0,1:T(8,128)S(1)} collective-permute-done((f32[32,768]{0,1:T(8,128)S(1)}, f32[32,768]{0,1:T(8,128)S(1)}, u32[]{:S(2)}, u32[]{:S(2)}) %collective-permute-start.1) | collective-permute-done | bytes 98336 | tf_op jit(solution)/shard_map/ppermute | solution.py:26
  26.3 1.9 %collective-permute-start.2 = (f32[192,32]{0,1:T(8,128)S(1)}, f32[192,32]{0,1:T(8,128)S(1)}, u32[]{:S(2)}, u32[]{:S(2)}) collective-permute-start(f32[192,32]{0,1:T(8,128)S(1)} %get-tuple-element.333), channel_id=1, source_target_pairs={{0,1},{1,2},{2,3},{3,4},{4,5},{5,6},{6,7},{8,9},{9,10},{10,11},{11... | collective-permute-start | bytes 73736 | tf_op jit(solution)/shard_map/ppermute | solution.py:25
  28.2 3.6 %collective-permute-start.3 = (f32[192,32]{0,1:T(8,128)S(1)}, f32[192,32]{0,1:T(8,128)S(1)}, u32[]{:S(2)}, u32[]{:S(2)}) collective-permute-start(f32[192,32]{0,1:T(8,128)S(1)} %get-tuple-element.334), channel_id=1, source_target_pairs={{1,0},{2,1},{3,2},{4,3},{5,4},{6,5},{7,6},{9,8},{10,9},{11,10},{12... | collective-permute-start | bytes 73736 | tf_op jit(solution)/shard_map/ppermute | solution.py:26
  31.9 1.5 %collective-permute-done.3 = f32[192,32]{0,1:T(8,128)S(1)} collective-permute-done((f32[192,32]{0,1:T(8,128)S(1)}, f32[192,32]{0,1:T(8,128)S(1)}, u32[]{:S(2)}, u32[]{:S(2)}) %collective-permute-start.3) | collective-permute-done | bytes 24608 | tf_op jit(solution)/shard_map/ppermute | solution.py:26
  33.8 3.0 %collective-permute-done.7 = f32[1,79,926]{1,2,0:T(8,128)} collective-permute-done((f32[1,79,926]{1,2,0:T(8,128)}, f32[1,79,926]{1,2,0:T(8,128)}, u32[]{:S(2)}, u32[]{:S(2)}) %collective-permute-start.7) | collective-permute-done | bytes 292648 | tf_op jit(solution)/shard_map/ppermute | solution.py:26
  36.8 1.6 %maximum_bitcast_fusion.5 = f32[286,926]{0,1:T(8,128)S(1)} fusion(f32[1,79,926]{1,2,0:T(8,128)} %collective-permute-done.7, f32[1,128,79]{1,2,0:T(8,128)S(1)} %collective-permute-done.5, f32[1,128,768]{1,2,0:T(8,128)S(1)} %bitcast.245, f32[1,128,79]{1,2,0:T(8,128)S(1)} %collective-permute-done.4, f32[1,79,926]{1,2,0:T(8,128)S(1)} %collective-permute-done.6), kind=kLoop, calls=%fused_computation.147 | loop fusion | flops 1059344 | bytes 2118688 | tf_op jit(solution)/shard_map/squeeze | solution.py:133
  38.4 97.0 %while.16 = (s32[]{:T(128)}, f32[2,12,128,128]{3,2,1,0:T(8,128)}, s32[2]{0:T(128)S(1)}, f32[192,832]{0,1:T(8,128)S(1)}, s32[2]{0:T(128)S(1)}, /*index=5*/s32[2]{...) while((s32[]{:T(128)}, f32[2,12,128,128]{3,2,1,0:T(8,128)}, ...), condition=%wide.region_4.5_spmd, body=%wide.region_0.4_spmd.sunk | while | flops 6243618816 | bytes 102016920 | solution.py:151
  43.0 0.8 fusion.238
  43.8 0.8 fusion.236
  47.2 0.8 fusion.230
  48.1 0.8 convolution_bitcast_fusion.7
  49.0 0.8 fusion.229
  49.8 0.8 fusion.231
  50.6 1.8 %fusion.234 = f32[12,192,192]{2,1,0:T(8,128)S(1)} fusion(f32[192,12,64]{0,2,1:T(8,128)S(1)} %get-tuple-element.397, f32[192,12,64]{0,2,1:T(8,128)S(1)} %get-tuple-element.398, f32[192,12,64]{0,2,1:T(8,128)S(1)} %get-tuple-element.399), kind=kOutput, calls=%fused_computation.47.clone.1 | convolution fusion | flops 510824448 | bytes 3538944 | tf_op jit(solution)/shard_map/while/body/eval_jaxpr/ua,nab->nub/dot_general | solution.py:70
  52.5 1.9 %fusion.232 = f32[12,192,192]{2,1,0:T(8,128)S(1)} fusion(f32[192,12,64]{0,2,1:T(8,128)S(1)} %get-tuple-element.397, f32[192,12,64]{0,2,1:T(8,128)S(1)} %get-tuple-element.398, f32[192,12,64]{0,2,1:T(8,128)S(1)} %get-tuple-element.399), kind=kOutput, calls=%fused_computation.46.clone.1 | convolution fusion | flops 510824448 | bytes 3538944 | tf_op jit(solution)/shard_map/while/body/eval_jaxpr/ua,nab->nub/dot_general | solution.py:71
  54.4 3.6 %fusion.240 = f32[12,192,192]{2,1,0:T(8,128)S(1)} fusion(f32[12,192,192]{2,1,0:T(8,128)S(1)} %fusion.232), kind=kOutput, calls=%fused_computation.1.clone.1 | convolution fusion | flops 510382080 | bytes 3538944 | tf_op jit(solution)/shard_map/while/body/eval_jaxpr/nub,vb->nuv/dot_general | solution.py:75
  58.0 3.0 %fusion.233 = f32[12,192,192]{2,1,0:T(8,128)S(1)} fusion(f32[12,192,192]{2,1,0:T(8,128)S(1)} %fusion.232), kind=kOutput, calls=%fused_computation.3.clone.1 | convolution fusion | flops 510382080 | bytes 3538944 | tf_op jit(solution)/shard_map/while/body/eval_jaxpr/nub,vb->nuv/dot_general | solution.py:72
  61.0 3.0 %fusion.235 = f32[12,192,192]{2,1,0:T(8,128)S(1)} fusion(f32[12,192,192]{2,1,0:T(8,128)S(1)} %fusion.233, f32[12,192,192]{2,1,0:T(8,128)S(1)} %fusion.234), kind=kOutput, calls=%fused_computation.17.clone.1 | convolution fusion | flops 510382080 | bytes 5308416 | tf_op jit(solution)/shard_map/while/body/eval_jaxpr/nub,vb->nuv/dot_general | solution.py:72
  64.0 3.0 %fusion.241 = f32[12,192,192]{2,1,0:T(8,128)S(1)} fusion(f32[12,192,192]{2,1,0:T(8,128)S(1)} %fusion.240, f32[12,192,192]{2,1,0:T(8,128)S(1)} %fusion.234), kind=kOutput, calls=%fused_computation.18.clone.1 | convolution fusion | flops 510382080 | bytes 5308416 | tf_op jit(solution)/shard_map/while/body/eval_jaxpr/nub,vb->nuv/dot_general | solution.py:75
  67.0 1.1 fusion.237
  68.2 1.3 convolution_add_fusion.3
  69.5 1.1 fusion.242
  70.6 1.5 %multiply_subtract_fusion.2 = (f32[12,192,192]{2,1,0:T(8,128)S(1)}, f32[12,192,192]{2,1,0:T(8,128)S(1)}) fusion(f32[12,192,192]{2,1,0:T(8,128)S(1)} %fusion.235, f32[12,192,192]{2,1,0:T(8,128)S(1)} %convolution_add_fusion.3, f32[12,192,192]{2,1,0:T(8,128)S(1)} %fusion.241, f32[12,192,192]{2,1,0:T(8,128)S(1)} %fusion.242, ...), kind=kOutput, calls=%fused_computation.11.clone.1 | convolution fusion | flops 342835200 | bytes 14254080 | tf_op jit(solution)/shard_map/while/body/eval_jaxpr/nub,vb->nuv/dot_general | solution.py:75
  72.1 2.4 %fusion.243 = f32[12,192,64]{2,1,0:T(8,128)S(1)} fusion(f32[12,192,192]{2,1,0:T(8,128)S(1)} %get-tuple-element.404, f32[192,192]{1,0:T(8,128)S(1)} %fusion.236), kind=kOutput, calls=%fused_computation.78.clone.1 | convolution fusion | flops 169869312 | bytes 3014656 | tf_op jit(solution)/shard_map/while/body/eval_jaxpr/pu,nuv->npv/dot_general | solution.py:91
  74.5 2.4 %fusion.244 = f32[12,64,192]{1,2,0:T(8,128)S(1)} fusion(f32[12,192,64]{2,1,0:T(8,128)S(1)} %fusion.243, f32[12,192,192]{2,1,0:T(8,128)S(1)} %get-tuple-element.405, f32[192,192]{1,0:T(8,128)S(1)} %fusion.238), kind=kOutput, calls=%fused_computation.22.clone.1 | convolution fusion | flops 170016768 | bytes 4194304 | tf_op jit(solution)/shard_map/while/body/eval_jaxpr/pu,nuv->npv/dot_general | solution.py:91
  76.9 2.4 %fusion.246 = f32[12,192,64]{2,1,0:T(8,128)S(1)} fusion(f32[12,192,192]{2,1,0:T(8,128)S(1)} %get-tuple-element.405, f32[192,192]{1,0:T(8,128)S(1)} %fusion.236), kind=kOutput, calls=%fused_computation.76.clone.1 | convolution fusion | flops 169869312 | bytes 3014656 | tf_op jit(solution)/shard_map/while/body/eval_jaxpr/pu,nuv->npv/dot_general | solution.py:94
  79.3 2.4 %fusion.247 = f32[12,64,192]{1,2,0:T(8,128)S(1)} fusion(f32[12,192,64]{2,1,0:T(8,128)S(1)} %fusion.246, f32[12,192,192]{2,1,0:T(8,128)S(1)} %get-tuple-element.404, f32[192,192]{1,0:T(8,128)S(1)} %fusion.238), kind=kOutput, calls=%fused_computation.20.clone.1 | convolution fusion | flops 170016768 | bytes 4194304 | tf_op jit(solution)/shard_map/while/body/eval_jaxpr/pu,nuv->npv/dot_general | solution.py:94
  81.8 1.2 fusion.245
  82.9 1.2 fusion.248
  84.6 0.8 fusion.250
  85.4 1.1 copy-done.1
  91.3 0.8 fusion.238
  92.1 0.8 fusion.236
  95.5 0.8 fusion.230
  96.4 0.8 convolution_bitcast_fusion.7
  97.2 0.8 fusion.229
  98.0 0.8 fusion.231
  98.9 1.8 %fusion.234 = f32[12,192,192]{2,1,0:T(8,128)S(1)} fusion(f32[192,12,64]{0,2,1:T(8,128)S(1)} %get-tuple-element.397, f32[192,12,64]{0,2,1:T(8,128)S(1)} %get-tuple-element.398, f32[192,12,64]{0,2,1:T(8,128)S(1)} %get-tuple-element.399), kind=kOutput, calls=%fused_computation.47.clone.1 | convolution fusion | flops 510824448 | bytes 3538944 | tf_op jit(solution)/shard_map/while/body/eval_jaxpr/ua,nab->nub/dot_general | solution.py:70
  100.7 1.9 %fusion.232 = f32[12,192,192]{2,1,0:T(8,128)S(1)} fusion(f32[192,12,64]{0,2,1:T(8,128)S(1)} %get-tuple-element.397, f32[192,12,64]{0,2,1:T(8,128)S(1)} %get-tuple-element.398, f32[192,12,64]{0,2,1:T(8,128)S(1)} %get-tuple-element.399), kind=kOutput, calls=%fused_computation.46.clone.1 | convolution fusion | flops 510824448 | bytes 3538944 | tf_op jit(solution)/shard_map/while/body/eval_jaxpr/ua,nab->nub/dot_general | solution.py:71
  102.6 3.2 %fusion.240 = f32[12,192,192]{2,1,0:T(8,128)S(1)} fusion(f32[12,192,192]{2,1,0:T(8,128)S(1)} %fusion.232), kind=kOutput, calls=%fused_computation.1.clone.1 | convolution fusion | flops 510382080 | bytes 3538944 | tf_op jit(solution)/shard_map/while/body/eval_jaxpr/nub,vb->nuv/dot_general | solution.py:75
  105.8 3.0 %fusion.233 = f32[12,192,192]{2,1,0:T(8,128)S(1)} fusion(f32[12,192,192]{2,1,0:T(8,128)S(1)} %fusion.232), kind=kOutput, calls=%fused_computation.3.clone.1 | convolution fusion | flops 510382080 | bytes 3538944 | tf_op jit(solution)/shard_map/while/body/eval_jaxpr/nub,vb->nuv/dot_general | solution.py:72
  108.8 3.0 %fusion.235 = f32[12,192,192]{2,1,0:T(8,128)S(1)} fusion(f32[12,192,192]{2,1,0:T(8,128)S(1)} %fusion.233, f32[12,192,192]{2,1,0:T(8,128)S(1)} %fusion.234), kind=kOutput, calls=%fused_computation.17.clone.1 | convolution fusion | flops 510382080 | bytes 5308416 | tf_op jit(solution)/shard_map/while/body/eval_jaxpr/nub,vb->nuv/dot_general | solution.py:72
  111.9 3.0 %fusion.241 = f32[12,192,192]{2,1,0:T(8,128)S(1)} fusion(f32[12,192,192]{2,1,0:T(8,128)S(1)} %fusion.240, f32[12,192,192]{2,1,0:T(8,128)S(1)} %fusion.234), kind=kOutput, calls=%fused_computation.18.clone.1 | convolution fusion | flops 510382080 | bytes 5308416 | tf_op jit(solution)/shard_map/while/body/eval_jaxpr/nub,vb->nuv/dot_general | solution.py:75
  114.9 1.1 fusion.237
  116.0 1.6 %convolution_add_fusion.3 = f32[12,192,192]{2,1,0:T(8,128)S(1)} fusion(f32[12,192,192]{2,1,0:T(8,128)S(1)} %fusion.237, f32[12,192,128]{2,1,0:T(8,128)S(1)} %fusion.239, f32[192,192]{1,0:T(8,128)S(1)} %fusion.238), kind=kOutput, calls=%fused_computation.16.clone.1 | convolution fusion | flops 340180992 | bytes 5406720 | tf_op jit(solution)/shard_map/while/body/eval_jaxpr/nub,vb->nuv/dot_general | solution.py:72
  117.6 1.1 fusion.242
  118.7 1.5 %multiply_subtract_fusion.2 = (f32[12,192,192]{2,1,0:T(8,128)S(1)}, f32[12,192,192]{2,1,0:T(8,128)S(1)}) fusion(f32[12,192,192]{2,1,0:T(8,128)S(1)} %fusion.235, f32[12,192,192]{2,1,0:T(8,128)S(1)} %convolution_add_fusion.3, f32[12,192,192]{2,1,0:T(8,128)S(1)} %fusion.241, f32[12,192,192]{2,1,0:T(8,128)S(1)} %fusion.242, ...), kind=kOutput, calls=%fused_computation.11.clone.1 | convolution fusion | flops 342835200 | bytes 14254080 | tf_op jit(solution)/shard_map/while/body/eval_jaxpr/nub,vb->nuv/dot_general | solution.py:75
  120.2 2.4 %fusion.243 = f32[12,192,64]{2,1,0:T(8,128)S(1)} fusion(f32[12,192,192]{2,1,0:T(8,128)S(1)} %get-tuple-element.404, f32[192,192]{1,0:T(8,128)S(1)} %fusion.236), kind=kOutput, calls=%fused_computation.78.clone.1 | convolution fusion | flops 169869312 | bytes 3014656 | tf_op jit(solution)/shard_map/while/body/eval_jaxpr/pu,nuv->npv/dot_general | solution.py:91
  122.6 2.4 %fusion.244 = f32[12,64,192]{1,2,0:T(8,128)S(1)} fusion(f32[12,192,64]{2,1,0:T(8,128)S(1)} %fusion.243, f32[12,192,192]{2,1,0:T(8,128)S(1)} %get-tuple-element.405, f32[192,192]{1,0:T(8,128)S(1)} %fusion.238), kind=kOutput, calls=%fused_computation.22.clone.1 | convolution fusion | flops 170016768 | bytes 4194304 | tf_op jit(solution)/shard_map/while/body/eval_jaxpr/pu,nuv->npv/dot_general | solution.py:91
  125.0 2.4 %fusion.246 = f32[12,192,64]{2,1,0:T(8,128)S(1)} fusion(f32[12,192,192]{2,1,0:T(8,128)S(1)} %get-tuple-element.405, f32[192,192]{1,0:T(8,128)S(1)} %fusion.236), kind=kOutput, calls=%fused_computation.76.clone.1 | convolution fusion | flops 169869312 | bytes 3014656 | tf_op jit(solution)/shard_map/while/body/eval_jaxpr/pu,nuv->npv/dot_general | solution.py:94
  127.4 2.4 %fusion.247 = f32[12,64,192]{1,2,0:T(8,128)S(1)} fusion(f32[12,192,64]{2,1,0:T(8,128)S(1)} %fusion.246, f32[12,192,192]{2,1,0:T(8,128)S(1)} %get-tuple-element.404, f32[192,192]{1,0:T(8,128)S(1)} %fusion.238), kind=kOutput, calls=%fused_computation.20.clone.1 | convolution fusion | flops 170016768 | bytes 4194304 | tf_op jit(solution)/shard_map/while/body/eval_jaxpr/pu,nuv->npv/dot_general | solution.py:94
  129.8 1.2 fusion.245
  131.0 1.2 fusion.248
  132.7 0.8 fusion.250
  133.5 1.1 copy-done.1
  (56 shorter events, 10.7 us)
Async XLA Ops:
  1.2 12.8 %collective-permute-start.4 = (f32[1,128,79]{1,2,0:T(8,128)S(1)}, f32[1,128,79]{1,2,0:T(8,128)S(1)}, u32[]{:S(2)}, u32[]{:S(2)}) collective-permute-start(f32[1,128,79]{1,2,0:T(8,128)S(1)} %get-tuple-element.337), channel_id=1, source_target_pairs={{0,1},{1,2},{2,3},{3,4},{4,5},{5,6},{6,7},{8,9},{9,10},{10,11},{11... | collective-permute-start | bytes 121352 | tf_op jit(solution)/shard_map/ppermute | solution.py:25
  3.1 10.9 %collective-permute-start.5 = (f32[1,128,79]{1,2,0:T(8,128)S(1)}, f32[1,128,79]{1,2,0:T(8,128)S(1)}, u32[]{:S(2)}, u32[]{:S(2)}) collective-permute-start(f32[1,128,79]{1,2,0:T(8,128)S(1)} %get-tuple-element.338), channel_id=1, source_target_pairs={{1,0},{2,1},{3,2},{4,3},{5,4},{6,5},{7,6},{9,8},{10,9},{11,10},{12... | collective-permute-start | bytes 121352 | tf_op jit(solution)/shard_map/ppermute | solution.py:26
  8.1 14.5 %collective-permute-start = (f32[32,768]{0,1:T(8,128)S(1)}, f32[32,768]{0,1:T(8,128)S(1)}, u32[]{:S(2)}, u32[]{:S(2)}) collective-permute-start(f32[32,768]{0,1:T(8,128)S(1)} %get-tuple-element.339), channel_id=1, source_target_pairs={{0,8},{8,16},{16,24},{24,32},{32,40},{40,48},{48,56},{56,64},{64,7... | collective-permute-start | bytes 294920 | tf_op jit(solution)/shard_map/ppermute | solution.py:25
  11.6 14.6 %collective-permute-start.1 = (f32[32,768]{0,1:T(8,128)S(1)}, f32[32,768]{0,1:T(8,128)S(1)}, u32[]{:S(2)}, u32[]{:S(2)}) collective-permute-start(f32[32,768]{0,1:T(8,128)S(1)} %get-tuple-element.340), channel_id=1, source_target_pairs={{8,0},{16,8},{24,16},{32,24},{40,32},{48,40},{56,48},{64,56},{72,6... | collective-permute-start | bytes 294920 | tf_op jit(solution)/shard_map/ppermute | solution.py:26
  15.1 18.7 %collective-permute-start.6 = (f32[1,79,926]{1,2,0:T(8,128)}, f32[1,79,926]{1,2,0:T(8,128)S(1)}, u32[]{:S(2)}, u32[]{:S(2)}) collective-permute-start(f32[1,79,926]{1,2,0:T(8,128)} %get-tuple-element.335), channel_id=1, source_target_pairs={{0,8},{8,16},{16,24},{24,32},{32,40},{40,48},{48,56},{56,64},{64,7... | collective-permute-start | bytes 877856 | tf_op jit(solution)/shard_map/ppermute | solution.py:25
  20.7 16.1 %collective-permute-start.7 = (f32[1,79,926]{1,2,0:T(8,128)}, f32[1,79,926]{1,2,0:T(8,128)}, u32[]{:S(2)}, u32[]{:S(2)}) collective-permute-start(f32[1,79,926]{1,2,0:T(8,128)} %get-tuple-element.336), channel_id=1, source_target_pairs={{8,0},{16,8},{24,16},{32,24},{40,32},{48,40},{56,48},{64,56},{72,6... | collective-permute-start | bytes 877856 | tf_op jit(solution)/shard_map/ppermute | solution.py:26
  26.3 5.6 %collective-permute-start.2 = (f32[192,32]{0,1:T(8,128)S(1)}, f32[192,32]{0,1:T(8,128)S(1)}, u32[]{:S(2)}, u32[]{:S(2)}) collective-permute-start(f32[192,32]{0,1:T(8,128)S(1)} %get-tuple-element.333), channel_id=1, source_target_pairs={{0,1},{1,2},{2,3},{3,4},{4,5},{5,6},{6,7},{8,9},{9,10},{10,11},{11... | collective-permute-start | bytes 73736 | tf_op jit(solution)/shard_map/ppermute | solution.py:25
  28.2 5.2 %collective-permute-start.3 = (f32[192,32]{0,1:T(8,128)S(1)}, f32[192,32]{0,1:T(8,128)S(1)}, u32[]{:S(2)}, u32[]{:S(2)}) collective-permute-start(f32[192,32]{0,1:T(8,128)S(1)} %get-tuple-element.334), channel_id=1, source_target_pairs={{1,0},{2,1},{3,2},{4,3},{5,4},{6,5},{7,6},{9,8},{10,9},{11,10},{12... | collective-permute-start | bytes 73736 | tf_op jit(solution)/shard_map/ppermute | solution.py:26
  31.9 6.5 %copy-start.2 = (s32[2]{0:T(128)S(1)}, s32[2]{0:T(128)}, u32[]{:S(2)}) copy-start(s32[2]{0:T(128)} %param.8) | copy-start | bytes 28
  31.9 6.5 %copy-start.3 = (s32[2]{0:T(128)S(1)}, s32[2]{0:T(128)}, u32[]{:S(2)}) copy-start(s32[2]{0:T(128)} %param.9) | copy-start | bytes 28
  81.7 2.8 %copy-start = (f32[2,12,128,128]{3,2,1,0:T(8,128)S(1)}, f32[2,12,128,128]{3,2,1,0:T(8,128)}, u32[]{:S(2)}) copy-start(f32[2,12,128,128]{3,2,1,0:T(8,128)} %get-tuple-element.428) | copy-start | bytes 4718596 | tf_op jit(solution)/shard_map/while
  85.4 1.1 copy-start.1
  129.8 2.8 %copy-start = (f32[2,12,128,128]{3,2,1,0:T(8,128)S(1)}, f32[2,12,128,128]{3,2,1,0:T(8,128)}, u32[]{:S(2)}) copy-start(f32[2,12,128,128]{3,2,1,0:T(8,128)} %get-tuple-element.428) | copy-start | bytes 4718596 | tf_op jit(solution)/shard_map/while
  133.5 1.1 copy-start.1
where the time goes:
time: 139 us; the launch traced here: 136 us
  matrix products  78.6 us (57%)
  starting transfers between devices  24.5 us (18%)
  local copies, waits for them, and re-layouts  11.1 us (8%)
  waiting for transfers between devices  8.1 us (6%)
  loops' own time  6.88 us (5%)
  other arithmetic  6.09 us (4%)
    ppermute x4, starting transfers between devices, extended(): before = lax.ppermute(last, axis, up)  12.9 us
    ppermute x4, starting transfers between devices, extended(): after = lax.ppermute(leading, axis, down)  11.6 us
    dot_general x4, matrix products, spectrum_of(): jnp.einsum('nub,vb->nuv', first_re, right_sin, precision=HIGH)  9.05 us
    dot_general x4, matrix products, spectrum_of(): jnp.einsum('nub,vb->nuv', first_im, right_cos, precision=HIGH)  9.01 us
    dot_general x4, matrix products, spectrum_of(): jnp.einsum('nub,vb->nuv', first_im, right_sin, precision=HIGH)  8.93 us
    dot_general x4, matrix products, spectrum_of(): jnp.einsum('nub,vb->nuv', first_re, right_cos, precision=HIGH)  8.27 us
    ppermute x4, waiting for transfers between devices, extended(): after = lax.ppermute(leading, axis, down)  8.09 us
    another operation x1, loops' own time, body(): return lax.map(one_row, (row_list, off_az, off_rg))  6.88 us
  transfers between devices with their start and end apart: 8, of which 3 were waited for; matrix products, arithmetic and copies ran while one was open for 2% of the time, Pallas kernels for 0%

commit v1 on v0

v1 whole, which is shorter than its diff:
```python
import functools

import jax
import jax.numpy as jnp
import numpy as np
from jax import lax
from jax.experimental import pallas as pl
from jax.experimental.pallas import tpu as pltpu
from jax.sharding import PartitionSpec as P

CHIP = 128
SPACE = 64
LAGS = 64
AREA = float(CHIP * CHIP)
EPSILON = 1e-06
ROWS = 128
COLS = 768
CHIPS = COLS // SPACE
PAIRS = CHIPS // 2
BLOCKS = CHIPS + 2
ROW_HALO = 80
REF_HALO = 32
LANE = 128
F32 = jnp.float32
BF16 = jnp.bfloat16


def halves(table):
    high = table.astype(jnp.bfloat16)
    low = (table - high.astype(np.float64)).astype(jnp.bfloat16)
    return high, low


def row_tables():
    freq = np.arange(64)[:, None] + 0.5
    out = []
    for j in range(4):
        angle = 2 * np.pi * freq * (64 * j + np.arange(64))[None, :] / 128
        high, low = halves(np.concatenate([np.cos(angle), -np.sin(angle)], axis=0))
        out.append(np.concatenate([high, high, low], axis=1))
    return np.stack(out)


def column_tables():
    angle = 2 * np.pi * np.arange(64)[:, None] * np.arange(128)[None, :] / 128
    c, s = np.cos(angle), np.sin(angle)
    sign = np.where(np.arange(256) % 2 == 0, 1.0, -1.0)[None, :]
    even = np.concatenate([np.concatenate([c, -s], 1), np.concatenate([s, c], 1)], 0)
    odd = np.concatenate([np.concatenate([s, c], 1), np.concatenate([c, -s], 1)], 0) * sign
    out = []
    for table in (even, odd):
        high, low = halves(table)
        out.append(np.concatenate([high, high, low], axis=0))
    return np.stack(out)


def back_tables():
    angle = 2 * np.pi * np.arange(64)[:, None] * (np.arange(64)[None, :] + 0.5) / 128
    c, s = np.cos(angle), np.sin(angle)
    high, low = halves(np.concatenate([np.concatenate([c, -s], 1), np.concatenate([s, c], 1)], 0))
    rows = np.concatenate([high, high, low], axis=1)
    angle = 2 * np.pi * np.arange(128)[:, None] * np.arange(64)[None, :] / 128
    high, low = halves(np.concatenate([np.cos(angle), -np.sin(angle)], 0) * (2.0 / AREA))
    none = np.zeros_like(high)
    first = np.concatenate([high, none, low, none], axis=1)
    second = np.concatenate([none, high, none, low], axis=1)
    return rows, np.stack([first, second])


def box_tables():
    lower = (np.arange(64)[None, :] < np.arange(64)[:, None]).astype(np.float64)
    none = np.zeros_like(lower)
    rows = np.concatenate(
        [np.concatenate([lower, lower, none, none], 1), np.concatenate([none, none, lower, lower], 1)], 0
    )
    cell = np.arange(256)[:, None]
    lag = np.arange(128)[None, :]
    start = np.where(lag < 64, lag, lag - 64 + 64)
    columns = ((cell >= start) & (cell < start + 128)).astype(np.float64)
    return rows.astype(jnp.bfloat16), columns.astype(jnp.bfloat16)


def cubic_tables():
    table = np.zeros((128, 64))
    for m in range(64):
        table[2 * m, m] = 1.0
        for step, weight in ((0, 9.0), (1, 9.0), (-1, -1.0), (2, -1.0)):
            table[2 * m + 1, min(max(m + step, 0), 63)] += weight / 16.0
    left = np.concatenate([table, table], axis=1)
    none = np.zeros((64, 128))
    right = np.concatenate(
        [np.concatenate([table.T, none], 1), np.concatenate([none, table.T], 1)], axis=0
    )
    return left.astype(jnp.bfloat16), right.astype(jnp.bfloat16)


def split(x):
    high = x.astype(BF16)
    return high, (x - high.astype(F32)).astype(BF16)


def dot(a, b):
    return jnp.dot(a, b, preferred_element_type=F32)


def shifted(x, shift, width):
    lane = lax.broadcasted_iota(jnp.int32, (x.shape[0], LANE), 1)
    turned = [
        pltpu.roll(x[:, i : i + LANE], LANE - shift, axis=1) for i in range(0, width + LANE, LANE)
    ]
    keep = lane < LANE - shift
    return jnp.concatenate(
        [jnp.where(keep, a, b) for a, b in zip(turned[:-1], turned[1:])], axis=1
    )


def lowered(x, shift):
    turn = lax.rem(8 - shift, 8)
    row = lax.broadcasted_iota(jnp.int32, (8, x.shape[1]), 0)
    turned = [pltpu.roll(x[i : i + 8], turn, axis=0) for i in range(0, 200, 8)]
    keep = row < 8 - shift
    return jnp.concatenate([jnp.where(keep, a, b) for a, b in zip(turned[:-1], turned[1:])], axis=0)


def range_spectra(rows_out, col_ref):
    lane = lax.broadcasted_iota(jnp.int32, (64, LANE), 1)
    low_half = lane < 64
    even, odd = [], []
    for x in rows_out:
        for i in range(0, x.shape[1], LANE):
            re = x[:64, i : i + LANE]
            im = pltpu.roll(x[64:, i : i + LANE], 64, axis=1)
            even.append(jnp.where(low_half, re, im))
            odd.append(jnp.where(low_half, im, re))
    out = []
    for parity, parts in enumerate((even, odd)):
        high, low = split(jnp.concatenate(parts, axis=0))
        got = dot(jnp.concatenate([high, low], axis=1), col_ref[parity, :256])
        got = got + dot(high, col_ref[parity, 256:])
        out.append(got)
    count = rows_out[0].shape[1] // LANE
    result = []
    for a in range(len(rows_out)):
        blocks = []
        for i in range(count):
            at = (a * count + i) * 64
            blocks += [out[0][at : at + 64], out[1][at : at + 64]]
        result.append(blocks)
    return result


def azimuth_spectra(x, row_ref, first):
    high, low = split(x)
    out = []
    for j in range(3):
        at = slice(64 * j, 64 * j + 64)
        stack = jnp.concatenate([high[at], low[at], high[at]], axis=0)
        out.append(dot(row_ref[first + j], stack))
    return out


def kernel(
    off_az,
    off_rg,
    ref_ref,
    sec_ref,
    row_ref,
    col_ref,
    back_row_ref,
    back_col_ref,
    box_row_ref,
    box_col_ref,
    up_left_ref,
    up_right_ref,
    out_ref,
    quads,
    windows,
    boxes,
    stats,
    strips,
    staged,
    sem,
):
    ref_mean = jnp.mean(ref_ref[REF_HALO : REF_HALO + ROWS, LANE : LANE + COLS], keepdims=True)
    sec_mean = jnp.mean(sec_ref[ROW_HALO : ROW_HALO + ROWS, LANE : LANE + COLS], keepdims=True)

    def reference_group(lane, width):
        x = ref_ref[:, pl.ds(lane, width + LANE)]
        x = shifted(x, LANE - REF_HALO, width) - ref_mean
        square = x * x
        sums = [jnp.sum(x[64 * m : 64 * m + 64], axis=0, keepdims=True) for m in range(3)]
        squares = [jnp.sum(square[64 * m : 64 * m + 64], axis=0, keepdims=True) for m in range(3)]
        rows = [sums[0] + sums[1], squares[0] + squares[1], sums[1] + sums[2], squares[1] + squares[2]]
        stats[:, pl.ds(lane, width)] = jnp.concatenate(rows + rows, axis=0)
        spectra = range_spectra(azimuth_spectra(x, row_ref, 0), col_ref)
        for m in range(3):
            for i, value in enumerate(spectra[m]):
                quads[m, lane // 64 + i] = value

    def window_group(k, lane, width):
        start = ROW_HALO - 64 + 64 * k + off_az[k]
        base = pl.multiple_of(start // 8 * 8, 8)
        w = sec_ref[pl.ds(base, 200), pl.ds(lane, width + LANE)]
        w = lowered(shifted(w, 64 + off_rg[k], width), start - base) - sec_mean
        parts = azimuth_spectra(w, row_ref, k)
        spectra = range_spectra([parts[0] + parts[1], parts[1] + parts[2]], col_ref)
        for m in range(2):
            for i, value in enumerate(spectra[m]):
                windows[k, m, lane // 64 + i] = value
        square = w * w
        tops = [
            jnp.broadcast_to(jnp.sum(v[:128], axis=0, keepdims=True), (64, width)) for v in (w, square)
        ]
        steps = [split(v[128:] - v[:64]) for v in (w, square)]
        stack = jnp.concatenate([steps[0][0], steps[0][1], steps[1][0], steps[1][1]], axis=0)
        boxes[k, :, pl.ds(lane, width)] = dot(box_row_ref[...], stack) + jnp.concatenate(tops, axis=0)

    def strip(k, n):
        re, im = 0.0, 0.0
        for m in range(2):
            q = quads[k + m, n]
            x = windows[k, m, n] + windows[k, m, n + 1]
            qr, qi, xr, xi = q[:, :128], q[:, 128:], x[:, :128], x[:, 128:]
            re = re + (qr * xr + qi * xi)
            im = im + (qr * xi - qi * xr)
        return jnp.concatenate([re, im], axis=0)

    def finish_pair(k, s):
        left = strips[k]
        middle = strip(k, 2 * s + 1)
        right = strip(k, 2 * s + 2)
        strips[k] = right
        high, low = split(jnp.concatenate([left + middle, middle + right], axis=1))
        y = dot(back_row_ref[:, :256], jnp.concatenate([high, low], axis=0))
        y = y + dot(back_row_ref[:, 256:], high)
        corr = 0.0
        for i in range(2):
            one = jnp.concatenate([y[:64, LANE * i : LANE * i + LANE], y[64:, LANE * i : LANE * i + LANE]], axis=1)
            high, low = split(one)
            wide = dot(high, back_col_ref[i])
            corr = corr + (wide[:, :128] + wide[:, 128:]) + dot(low, back_col_ref[i, :, :128])
        lane = s * LANE if isinstance(s, int) else pl.multiple_of(s * LANE, LANE)
        high, low = split(boxes[k, :, pl.ds(lane, 256)])
        box = dot(high, box_col_ref[...]) + dot(low, box_col_ref[...])
        first, second = box[:64], box[64:]
        stat = stats[:, pl.ds(lane, 256)]
        place = lax.broadcasted_iota(jnp.int32, stat.shape, 1)
        a = jnp.sum(stat[:, :128], axis=1, keepdims=True)
        b = jnp.sum(jnp.where((place >= 64) & (place < 192), stat, 0.0), axis=1, keepdims=True)
        both = jnp.where(place[:, :128] < 64, a, b)
        total, power = both[2 * k : 2 * k + 1], both[2 * k + 1 : 2 * k + 2]
        mean = total / AREA
        energy = power - total * mean
        centered = corr - mean * first
        var_sum = jnp.maximum(second - first * first / AREA, 0.0)
        score = (CHIP / AREA) * centered * lax.rsqrt((energy / AREA) * (var_sum / AREA) + EPSILON)
        high, low = split(score)
        lifted = dot(up_left_ref[...], jnp.concatenate([high, low], axis=0))
        high, low = split(lifted)
        both = dot(high, up_right_ref[...]) + dot(low, up_right_ref[...])
        at = k * CHIPS + 2 * s
        staged[at] = both[:, :128]
        staged[at + 1] = both[:, 128:]
        pltpu.make_async_copy(staged.at[pl.ds(at, 2)], out_ref.at[pl.ds(at, 2)], sem).start()

    def group(g, carry):
        lane = pl.multiple_of(g * 256, 256)
        reference_group(lane, 256)
        for k in range(2):
            window_group(k, lane, 256)
        return carry

    lax.fori_loop(0, 3, group, 0)
    reference_group(768, 128)
    for k in range(2):
        window_group(k, 768, 128)

    for k in range(2):
        strips[k] = strip(k, 0)

    def pair(s, carry):
        for k in range(2):
            finish_pair(k, s)
        return carry

    lax.fori_loop(0, PAIRS, pair, 0)
    pltpu.make_async_copy(staged, out_ref, sem).wait()


def extended(value, sides):
    for axis, dim, width in sides:
        size, length = lax.axis_size(axis), value.shape[dim]
        up = [(i, i + 1) for i in range(size - 1)]
        down = [(j, i) for i, j in up]
        last = lax.slice_in_dim(value, length - width, length, axis=dim)
        leading = lax.slice_in_dim(value, 0, width, axis=dim)
        before = lax.ppermute(last, axis, up)
        after = lax.ppermute(leading, axis, down)
        value = jnp.concatenate([before, value, after], axis=dim)
    return value


def body(ref_image, sec_image, off_az, off_rg):
    ref_ext = extended(ref_image, (("az", 0, REF_HALO), ("rg", 1, LANE)))
    sec_ext = extended(sec_image, (("az", 0, ROW_HALO), ("rg", 1, LANE)))
    back_rows, back_cols = back_tables()
    box_rows, box_cols = box_tables()
    left, right = cubic_tables()
    tables = [row_tables(), column_tables(), back_rows, back_cols, box_rows, box_cols, left, right]
    vmem = pl.BlockSpec(memory_space=pltpu.VMEM)
    smem = pl.BlockSpec(memory_space=pltpu.SMEM)
    out = pl.pallas_call(
        kernel,
        out_shape=jax.ShapeDtypeStruct((2 * CHIPS, 128, 128), F32),
        in_specs=[smem, smem] + [vmem] * 10,
        out_specs=pl.BlockSpec(memory_space=pl.ANY),
        scratch_shapes=[
            pltpu.VMEM((3, BLOCKS, 64, 256), F32),
            pltpu.VMEM((2, 2, BLOCKS, 64, 256), F32),
            pltpu.VMEM((2, 128, BLOCKS * 64), F32),
            pltpu.VMEM((8, BLOCKS * 64), F32),
            pltpu.VMEM((2, 128, 128), F32),
            pltpu.VMEM((2 * CHIPS, 128, 128), F32),
            pltpu.SemaphoreType.DMA,
        ],
    )(off_az, off_rg, ref_ext, sec_ext, *[jnp.asarray(t) for t in tables])
    return out.reshape(2, CHIPS, 128, 128)


def solution(mesh):
    return jax.shard_map(
        body,
        mesh=mesh,
        in_specs=(P("az", "rg"), P("az", "rg"), P("az"), P("az")),
        out_specs=P("az", "rg", None, None),
        check_vma=False,
    )
```

time: 139 us -> 53.2 us (0.38)
  the two profiles are of different devices: /device:TPU:26 before, /device:TPU:99 now
where the time goes in v1:
time: 53.2 us; the launch traced here: 52.8 us
  starting transfers between devices  27.7 us (52%)
  Pallas kernels  15.5 us (29%)
  waiting for transfers between devices  5.02 us (9%)
  local copies, waits for them, and re-layouts  2.26 us (4%)
  other arithmetic  2.15 us (4%)
    pallas_call x1, Pallas kernels, body(): pl.pallas_call(kernel, out_shape=jax.ShapeDtypeStruct((2 * CHIPS, 128, 12...  15.5 us
    ppermute x4, starting transfers between devices, extended(): after = lax.ppermute(leading, axis, down)  13.9 us
    ppermute x4, starting transfers between devices, extended(): before = lax.ppermute(last, axis, up)  13.7 us
    ppermute x4, waiting for transfers between devices, extended(): after = lax.ppermute(leading, axis, down)  3.52 us
    concatenate x2, other arithmetic, extended(): value = jnp.concatenate([before, value, after], axis=dim)  2.15 us
    slice x2, local copies, waits for them, and re-layouts, extended(): leading = lax.slice_in_dim(value, 0, width, axis=dim)  2.1 us
    ppermute x4, waiting for transfers between devices, extended(): before = lax.ppermute(last, axis, up)  1.5 us
  transfers between devices with their start and end apart: 8, of which 2 were waited for; matrix products, arithmetic and copies ran while one was open for 4% of the time, Pallas kernels for 0%

profile of v1, /device:TPU:99, one launch (start us, length us, event | category | flops | bytes accessed | tf_op | source)
XLA Modules:
  0.0 52.8 jit_solution(718024753162179685)
XLA Ops:
  0.0 0.0 copy-start.1
  0.0 1.0 %fusion.3 = (f32[32,768]{1,0:T(8,128)S(1)}, f32[32,768]{1,0:T(8,128)S(1)}) fusion(f32[128,768]{1,0:T(8,128)} %param.12), kind=kLoop, calls=%fused_computation.11 | loop fusion | bytes 393216 | tf_op jit(solution)/shard_map/slice | solution.py:296
  1.0 4.5 %collective-permute-start.1 = (f32[32,768]{1,0:T(8,128)S(1)}, f32[32,768]{1,0:T(8,128)S(1)}, u32[]{:S(2)}, u32[]{:S(2)}) collective-permute-start(f32[32,768]{1,0:T(8,128)S(1)} %get-tuple-element.11), channel_id=1, source_target_pairs={{8,0},{16,8},{24,16},{32,24},{40,32},{48,40},{56,48},{64,56},{72,6... | collective-permute-start | bytes 294920 | tf_op jit(solution)/shard_map/ppermute | solution.py:298
  5.5 1.9 %collective-permute-start = (f32[32,768]{1,0:T(8,128)S(1)}, f32[32,768]{1,0:T(8,128)S(1)}, u32[]{:S(2)}, u32[]{:S(2)}) collective-permute-start(f32[32,768]{1,0:T(8,128)S(1)} %get-tuple-element.12), channel_id=1, source_target_pairs={{0,8},{8,16},{16,24},{24,32},{32,40},{40,48},{48,56},{56,64},{64,7... | collective-permute-start | bytes 294920 | tf_op jit(solution)/shard_map/ppermute | solution.py:297
  7.4 1.1 %fusion.2 = (f32[80,768]{1,0:T(8,128)S(1)}, f32[80,768]{1,0:T(8,128)S(1)}) fusion(f32[128,768]{1,0:T(8,128)} %param.13), kind=kLoop, calls=%fused_computation.10 | loop fusion | bytes 983040 | tf_op jit(solution)/shard_map/slice | solution.py:296
  8.5 0.0 copy-start
  8.5 5.6 %collective-permute-start.5 = (f32[80,768]{1,0:T(8,128)S(1)}, f32[80,768]{1,0:T(8,128)S(1)}, u32[]{:S(2)}, u32[]{:S(2)}) collective-permute-start(f32[80,768]{1,0:T(8,128)S(1)} %get-tuple-element.9), channel_id=1, source_target_pairs={{8,0},{16,8},{24,16},{32,24},{40,32},{48,40},{56,48},{64,56},{72,6... | collective-permute-start | bytes 737288 | tf_op jit(solution)/shard_map/ppermute | solution.py:298
  14.2 1.9 %collective-permute-start.4 = (f32[80,768]{1,0:T(8,128)S(1)}, f32[80,768]{1,0:T(8,128)S(1)}, u32[]{:S(2)}, u32[]{:S(2)}) collective-permute-start(f32[80,768]{1,0:T(8,128)S(1)} %get-tuple-element.10), channel_id=1, source_target_pairs={{0,8},{8,16},{16,24},{24,32},{32,40},{40,48},{48,56},{56,64},{64,7... | collective-permute-start | bytes 737288 | tf_op jit(solution)/shard_map/ppermute | solution.py:297
  16.1 0.0 collective-permute-done
  16.1 0.0 copy-done.1
  16.2 0.0 collective-permute-done.1
  16.2 4.5 %collective-permute-start.2 = (f32[192,128]{1,0:T(8,128)S(1)}, f32[192,128]{1,0:T(8,128)S(1)}, u32[]{:S(2)}, u32[]{:S(2)}) collective-permute-start(f32[192,128]{1,0:T(8,128)S(1)} %get-tuple-element.7), channel_id=1, source_target_pairs={{0,1},{1,2},{2,3},{3,4},{4,5},{5,6},{6,7},{8,9},{9,10},{10,11},{11... | collective-permute-start | bytes 294920 | tf_op jit(solution)/shard_map/ppermute | solution.py:297
  20.7 1.9 %collective-permute-start.3 = (f32[192,128]{1,0:T(8,128)S(1)}, f32[192,128]{1,0:T(8,128)S(1)}, u32[]{:S(2)}, u32[]{:S(2)}) collective-permute-start(f32[192,128]{1,0:T(8,128)S(1)} %get-tuple-element.8), channel_id=1, source_target_pairs={{1,0},{2,1},{3,2},{4,3},{5,4},{6,5},{7,6},{9,8},{10,9},{11,10},{12... | collective-permute-start | bytes 294920 | tf_op jit(solution)/shard_map/ppermute | solution.py:298
  22.7 1.5 %collective-permute-done.4 = f32[80,768]{1,0:T(8,128)S(1)} collective-permute-done((f32[80,768]{1,0:T(8,128)S(1)}, f32[80,768]{1,0:T(8,128)S(1)}, u32[]{:S(2)}, u32[]{:S(2)}) %collective-permute-start.4) | collective-permute-done | bytes 245792 | tf_op jit(solution)/shard_map/ppermute | solution.py:297
  24.2 0.0 copy-done
  24.2 0.0 collective-permute-done.5
  24.3 5.4 %collective-permute-start.6 = (f32[288,128]{1,0:T(8,128)S(1)}, f32[288,128]{1,0:T(8,128)S(1)}, u32[]{:S(2)}, u32[]{:S(2)}) collective-permute-start(f32[288,128]{1,0:T(8,128)S(1)} %get-tuple-element.5), channel_id=1, source_target_pairs={{0,1},{1,2},{2,3},{3,4},{4,5},{5,6},{6,7},{8,9},{9,10},{10,11},{11... | collective-permute-start | bytes 442376 | tf_op jit(solution)/shard_map/ppermute | solution.py:297
  29.7 1.9 %collective-permute-start.7 = (f32[288,128]{1,0:T(8,128)S(1)}, f32[288,128]{1,0:T(8,128)S(1)}, u32[]{:S(2)}, u32[]{:S(2)}) collective-permute-start(f32[288,128]{1,0:T(8,128)S(1)} %get-tuple-element.6), channel_id=1, source_target_pairs={{1,0},{2,1},{3,2},{4,3},{5,4},{6,5},{7,6},{9,8},{10,9},{11,10},{12... | collective-permute-start | bytes 442376 | tf_op jit(solution)/shard_map/ppermute | solution.py:298
  31.6 0.0 collective-permute-done.2
  31.6 0.0 collective-permute-done.3
  31.6 1.0 %pad_maximum_fusion.1.ref_ref = f32[192,1024]{1,0:T(8,128)} fusion(f32[192,128]{1,0:T(8,128)S(1)} %collective-permute-done.3, f32[192,768]{1,0:T(8,128)S(1)} %constant_dynamic-update-slice_fusion, f32[192,128]{1,0:T(8,128)S(1)} %collective-permute-done.2), kind=kLoop, calls=%fused_computation.1 | loop fusion | flops 393216 | bytes 1572864 | tf_op jit(solution)/shard_map/concatenate | solution.py:299
  32.6 0.0 collective-permute-done.6
  32.6 3.5 %collective-permute-done.7 = f32[288,128]{1,0:T(8,128)S(1)} collective-permute-done((f32[288,128]{1,0:T(8,128)S(1)}, f32[288,128]{1,0:T(8,128)S(1)}, u32[]{:S(2)}, u32[]{:S(2)}) %collective-permute-start.7) | collective-permute-done | bytes 147488 | tf_op jit(solution)/shard_map/ppermute | solution.py:298
  36.1 1.2 %pad_maximum_fusion.sec_ref = f32[288,1024]{1,0:T(8,128)} fusion(f32[288,128]{1,0:T(8,128)S(1)} %collective-permute-done.7, f32[288,768]{1,0:T(8,128)S(1)} %constant_dynamic-update-slice_fusion.3, f32[288,128]{1,0:T(8,128)S(1)} %collective-permute-done.6), kind=kLoop, calls=%fused_computation | loop fusion | flops 589824 | bytes 2359296 | tf_op jit(solution)/shard_map/concatenate | solution.py:299
  37.3 15.5 %shard_map.118 = f32[24,128,128]{2,1,0:T(8,128)} custom-call(s32[2]{0:T(128)} %off_az.1, s32[2]{0:T(128)} %off_rg.1, f32[192,1024]{1,0:T(8,128)} %pad_maximum_fusion.1.ref_ref, f32[288,1024]{1,0:T(8,128)} %pad_maximum_fusion.sec_ref, bf16[4,128,192]{2,1,0:T(8,128)(2,1)} %constant.16.clone.row_ref, bf16[2,384,256]{2,1,0:T(8,128)(2,1)} %constant.17.clone.col_ref, ...), custom_call_target="tpu_custom_call" | custom-call | tf_op jit(solution)/shard_map/pallas_call | solution.py:312
  (8 shorter events, 0.1 us)
Async XLA Ops:
  0.0 16.1 %copy-start.1 = (f32[128,768]{1,0:T(8,128)S(1)}, f32[128,768]{1,0:T(8,128)}, u32[]{:S(2)}) copy-start(f32[128,768]{1,0:T(8,128)} %param.12) | copy-start | bytes 1179652
  1.0 15.1 %collective-permute-start.1 = (f32[32,768]{1,0:T(8,128)S(1)}, f32[32,768]{1,0:T(8,128)S(1)}, u32[]{:S(2)}, u32[]{:S(2)}) collective-permute-start(f32[32,768]{1,0:T(8,128)S(1)} %get-tuple-element.11), channel_id=1, source_target_pairs={{8,0},{16,8},{24,16},{32,24},{40,32},{48,40},{56,48},{64,56},{72,6... | collective-permute-start | bytes 294920 | tf_op jit(solution)/shard_map/ppermute | solution.py:298
  5.5 10.6 %collective-permute-start = (f32[32,768]{1,0:T(8,128)S(1)}, f32[32,768]{1,0:T(8,128)S(1)}, u32[]{:S(2)}, u32[]{:S(2)}) collective-permute-start(f32[32,768]{1,0:T(8,128)S(1)} %get-tuple-element.12), channel_id=1, source_target_pairs={{0,8},{8,16},{16,24},{24,32},{32,40},{40,48},{48,56},{56,64},{64,7... | collective-permute-start | bytes 294920 | tf_op jit(solution)/shard_map/ppermute | solution.py:297
  8.5 15.6 %copy-start = (f32[128,768]{1,0:T(8,128)S(1)}, f32[128,768]{1,0:T(8,128)}, u32[]{:S(2)}) copy-start(f32[128,768]{1,0:T(8,128)} %param.13) | copy-start | bytes 1179652
  8.5 15.7 %collective-permute-start.5 = (f32[80,768]{1,0:T(8,128)S(1)}, f32[80,768]{1,0:T(8,128)S(1)}, u32[]{:S(2)}, u32[]{:S(2)}) collective-permute-start(f32[80,768]{1,0:T(8,128)S(1)} %get-tuple-element.9), channel_id=1, source_target_pairs={{8,0},{16,8},{24,16},{32,24},{40,32},{48,40},{56,48},{64,56},{72,6... | collective-permute-start | bytes 737288 | tf_op jit(solution)/shard_map/ppermute | solution.py:298
  14.2 10.0 %collective-permute-start.4 = (f32[80,768]{1,0:T(8,128)S(1)}, f32[80,768]{1,0:T(8,128)S(1)}, u32[]{:S(2)}, u32[]{:S(2)}) collective-permute-start(f32[80,768]{1,0:T(8,128)S(1)} %get-tuple-element.10), channel_id=1, source_target_pairs={{0,8},{8,16},{16,24},{24,32},{32,40},{40,48},{48,56},{56,64},{64,7... | collective-permute-start | bytes 737288 | tf_op jit(solution)/shard_map/ppermute | solution.py:297
  16.2 15.4 %collective-permute-start.2 = (f32[192,128]{1,0:T(8,128)S(1)}, f32[192,128]{1,0:T(8,128)S(1)}, u32[]{:S(2)}, u32[]{:S(2)}) collective-permute-start(f32[192,128]{1,0:T(8,128)S(1)} %get-tuple-element.7), channel_id=1, source_target_pairs={{0,1},{1,2},{2,3},{3,4},{4,5},{5,6},{6,7},{8,9},{9,10},{10,11},{11... | collective-permute-start | bytes 294920 | tf_op jit(solution)/shard_map/ppermute | solution.py:297
  20.7 10.9 %collective-permute-start.3 = (f32[192,128]{1,0:T(8,128)S(1)}, f32[192,128]{1,0:T(8,128)S(1)}, u32[]{:S(2)}, u32[]{:S(2)}) collective-permute-start(f32[192,128]{1,0:T(8,128)S(1)} %get-tuple-element.8), channel_id=1, source_target_pairs={{1,0},{2,1},{3,2},{4,3},{5,4},{6,5},{7,6},{9,8},{10,9},{11,10},{12... | collective-permute-start | bytes 294920 | tf_op jit(solution)/shard_map/ppermute | solution.py:298
  24.3 8.3 %collective-permute-start.6 = (f32[288,128]{1,0:T(8,128)S(1)}, f32[288,128]{1,0:T(8,128)S(1)}, u32[]{:S(2)}, u32[]{:S(2)}) collective-permute-start(f32[288,128]{1,0:T(8,128)S(1)} %get-tuple-element.5), channel_id=1, source_target_pairs={{0,1},{1,2},{2,3},{3,4},{4,5},{5,6},{6,7},{8,9},{9,10},{10,11},{11... | collective-permute-start | bytes 442376 | tf_op jit(solution)/shard_map/ppermute | solution.py:297
  29.7 6.5 %collective-permute-start.7 = (f32[288,128]{1,0:T(8,128)S(1)}, f32[288,128]{1,0:T(8,128)S(1)}, u32[]{:S(2)}, u32[]{:S(2)}) collective-permute-start(f32[288,128]{1,0:T(8,128)S(1)} %get-tuple-element.6), channel_id=1, source_target_pairs={{1,0},{2,1},{3,2},{4,3},{5,4},{6,5},{7,6},{9,8},{10,9},{11,10},{12... | collective-permute-start | bytes 442376 | tf_op jit(solution)/shard_map/ppermute | solution.py:298

commit v2 on v1

v2 whole, which is shorter than its diff:
```python
import functools

import jax
import jax.numpy as jnp
import numpy as np
from jax import lax
from jax.experimental import pallas as pl
from jax.experimental.pallas import tpu as pltpu
from jax.sharding import PartitionSpec as P

CHIP = 128
SPACE = 64
LAGS = 64
AREA = float(CHIP * CHIP)
EPSILON = 1e-06
ROWS = 128
COLS = 768
CHIPS = COLS // SPACE
PAIRS = CHIPS // 2
BLOCKS = CHIPS + 2
WIDE = BLOCKS * SPACE
ROW_HALO = 80
REF_HALO = 32
NEAR = 16
FAR = 64
REACH = 160
LANE = 128
MESH = pl.DeviceIdType.MESH
F32 = jnp.float32
BF16 = jnp.bfloat16


def halves(table):
    high = table.astype(jnp.bfloat16)
    low = (table - high.astype(np.float64)).astype(jnp.bfloat16)
    return high, low


def azimuth_table(first, count):
    angle = 2 * np.pi * (np.arange(64)[:, None] + 0.5) * (first + np.arange(count))[None, :] / 128
    high, low = halves(np.concatenate([np.cos(angle), -np.sin(angle)], axis=0))
    return np.concatenate([high, high, low], axis=1)


def box_table():
    cell = np.arange(256)[:, None]
    lag = np.arange(128)[None, :]
    return ((cell >= lag) & (cell < lag + 128)).astype(jnp.bfloat16)


def column_tables():
    angle = 2 * np.pi * np.arange(64)[:, None] * np.arange(128)[None, :] / 128
    c, s = np.cos(angle), np.sin(angle)
    sign = np.where(np.arange(256) % 2 == 0, 1.0, -1.0)[None, :]
    even = np.concatenate([np.concatenate([c, -s], 1), np.concatenate([s, c], 1)], 0)
    odd = np.concatenate([np.concatenate([s, c], 1), np.concatenate([c, -s], 1)], 0) * sign
    out = []
    for table in (even, odd):
        high, low = halves(table)
        out.append(np.concatenate([high, high, low], axis=0))
    return np.stack(out)


def back_tables():
    angle = 2 * np.pi * np.arange(64)[:, None] * (np.arange(64)[None, :] + 0.5) / 128
    c, s = np.cos(angle), np.sin(angle)
    high, low = halves(np.concatenate([np.concatenate([c, -s], 1), np.concatenate([s, c], 1)], 0))
    rows = np.concatenate([high, high, low], axis=1)
    angle = 2 * np.pi * np.arange(128)[:, None] * np.arange(64)[None, :] / 128
    high, low = halves(np.concatenate([np.cos(angle), -np.sin(angle)], 0) * (2.0 / AREA))
    none = np.zeros_like(high)
    first = np.concatenate([high, none, low, none], axis=1)
    second = np.concatenate([none, high, none, low], axis=1)
    return rows, np.stack([first, second])


def cubic_tables():
    table = np.zeros((128, 64))
    for m in range(64):
        table[2 * m, m] = 1.0
        for step, weight in ((0, 9.0), (1, 9.0), (-1, -1.0), (2, -1.0)):
            table[2 * m + 1, min(max(m + step, 0), 63)] += weight / 16.0
    left = np.concatenate([table, table], axis=1)
    none = np.zeros((64, 128))
    right = np.concatenate(
        [np.concatenate([table.T, none], 1), np.concatenate([none, table.T], 1)], axis=0
    )
    return left.astype(jnp.bfloat16), right.astype(jnp.bfloat16)


def split(x):
    high = x.astype(BF16)
    return high, (x - high.astype(F32)).astype(BF16)


def dot(a, b):
    return jnp.dot(a, b, preferred_element_type=F32)


def shifted(x, shift, width):
    lane = lax.broadcasted_iota(jnp.int32, (x.shape[0], LANE), 1)
    turned = [
        pltpu.roll(x[:, i : i + LANE], LANE - shift, axis=1) for i in range(0, width + LANE, LANE)
    ]
    keep = lane < LANE - shift
    return jnp.concatenate(
        [jnp.where(keep, a, b) for a, b in zip(turned[:-1], turned[1:])], axis=1
    )


def range_spectra(rows_out, col_ref):
    lane = lax.broadcasted_iota(jnp.int32, (64, LANE), 1)
    low_half = lane < 64
    even, odd = [], []
    for x in rows_out:
        for i in range(0, x.shape[1], LANE):
            re = x[:64, i : i + LANE]
            im = pltpu.roll(x[64:, i : i + LANE], 64, axis=1)
            even.append(jnp.where(low_half, re, im))
            odd.append(jnp.where(low_half, im, re))
    out = []
    for parity, parts in enumerate((even, odd)):
        high, low = split(jnp.concatenate(parts, axis=0))
        got = dot(jnp.concatenate([high, low], axis=1), col_ref[parity, :256])
        got = got + dot(high, col_ref[parity, 256:])
        out.append(got)
    count = rows_out[0].shape[1] // LANE
    result = []
    for a in range(len(rows_out)):
        blocks = []
        for i in range(count):
            at = (a * count + i) * 64
            blocks += [out[0][at : at + 64], out[1][at : at + 64]]
        result.append(blocks)
    return result


def ones_where(condition):
    return jnp.where(condition, 1.0, 0.0).astype(BF16)


class Exchange:
    def __init__(self, tiles, bufs, tile_sems, send_sems, recv_sems):
        az, rg = lax.axis_index("az"), lax.axis_index("rg")
        last_az, last_rg = lax.axis_size("az") - 1, lax.axis_size("rg") - 1
        self.up = ("az", az - 1, az > 0)
        self.down = ("az", az + 1, az < last_az)
        self.left = ("rg", rg - 1, rg > 0)
        self.right = ("rg", rg + 1, rg < last_rg)
        self.sides = (self.up, self.down, self.left, self.right)
        self.bufs, self.send_sems, self.recv_sems, self.count = bufs, send_sems, recv_sems, 0
        self.all = []
        self.loads = []
        for i, (tile, (buf, halo)) in enumerate(zip(tiles, bufs)):
            own = buf.at[pl.ds(halo, ROWS), pl.ds(LANE, COLS)]
            self.loads.append(pltpu.make_async_copy(tile, own, tile_sems.at[i]))

    def greet(self):
        for load in self.loads:
            load.start()
        barrier = pltpu.get_barrier_semaphore()
        for axis, place, there in self.sides:

            @pl.when(there)
            def _(axis=axis, place=place):
                pl.semaphore_signal(barrier, inc=1, device_id={axis: place}, device_id_type=MESH)

    def clear(self):
        up, down, left, right = self.sides
        for buf, halo in self.bufs:
            for side, rows, lanes in (
                (up, slice(0, halo), slice(None)),
                (down, slice(halo + ROWS, 2 * halo + ROWS), slice(None)),
                (left, slice(None), slice(0, LANE)),
                (right, slice(None), slice(LANE + COLS, 2 * LANE + COLS)),
            ):

                @pl.when(jnp.logical_not(side[2]))
                def _(buf=buf, rows=rows, lanes=lanes):
                    shape = [n if c == slice(None) else c.stop - c.start for n, c in zip(buf.shape, (rows, lanes))]
                    buf[rows, lanes] = jnp.zeros(shape, F32)

    def meet(self):
        barrier = pltpu.get_barrier_semaphore()
        peers = sum(there.astype(jnp.int32) for _, _, there in self.sides)
        pl.semaphore_wait(barrier, peers)

    def copy(self, buf, rows, lanes, to_rows, to_lanes, side, back, have=None):
        index = self.count
        self.count += 1
        axis, place, sends = side
        comes = back[2]
        if have is not None:
            sends, comes = sends & have, comes & have
        transfer = pltpu.make_async_remote_copy(
            src_ref=buf.at[pl.ds(*rows), pl.ds(*lanes)],
            dst_ref=buf.at[pl.ds(*to_rows), pl.ds(*to_lanes)],
            send_sem=self.send_sems.at[index],
            recv_sem=self.recv_sems.at[index],
            device_id={axis: place},
            device_id_type=MESH,
        )
        entry = (transfer, sends, comes)
        self.all.append(entry)
        return entry

    def along_azimuth(self, buf, halo, near, far, lanes):
        count = far - near
        end = halo + ROWS
        return [
            self.copy(buf, (halo + near, count), lanes, (end + near, count), lanes, self.up, self.down),
            self.copy(buf, (end - far, count), lanes, (halo - far, count), lanes, self.down, self.up),
        ]

    def along_range(self, buf, rows, have=None):
        return [
            self.copy(buf, rows, (LANE, LANE), rows, (LANE + COLS, LANE), self.left, self.right, have),
            self.copy(buf, rows, (COLS, LANE), rows, (0, LANE), self.right, self.left, have),
        ]

    def corners(self, buf, halo, near, far):
        count = far - near
        return self.along_range(buf, (halo - far, count), self.up[2]) + self.along_range(
            buf, (halo + ROWS + near, count), self.down[2]
        )

    @staticmethod
    def start(entries):
        for transfer, sends, _ in entries:

            @pl.when(sends)
            def _(transfer=transfer):
                transfer.start()

    @staticmethod
    def arrive(entries):
        for transfer, _, comes in entries:

            @pl.when(comes)
            def _(transfer=transfer):
                transfer.wait_recv()

    def close(self):
        for transfer, sends, _ in self.all:

            @pl.when(sends)
            def _(transfer=transfer):
                transfer.wait_send()


def kernel(
    off_az,
    off_rg,
    ref_tile,
    sec_tile,
    ref_row_ref,
    sec_row_ref,
    col_ref,
    back_row_ref,
    back_col_ref,
    box_col_ref,
    up_left_ref,
    up_right_ref,
    out_ref,
    ref_buf,
    sec_buf,
    row_mats,
    box_mid,
    box_far,
    sec_high,
    sec_low,
    quads,
    windows,
    boxes,
    stats,
    strips,
    staged,
    sem,
    tile_sems,
    send_sems,
    recv_sems,
):
    halo = Exchange(
        (ref_tile, sec_tile),
        ((ref_buf, REF_HALO), (sec_buf, ROW_HALO)),
        tile_sems,
        send_sems,
        recv_sems,
    )
    everything = (LANE, COLS)
    near = halo.along_azimuth(sec_buf, ROW_HALO, 0, NEAR, everything)
    beside = halo.along_range(sec_buf, (ROW_HALO, ROWS)) + halo.along_range(ref_buf, (REF_HALO, ROWS))
    far = {}
    order = (1, 6, 2, 5, 3, 4)
    for b in order:
        lanes = (LANE * b, LANE)
        far[b] = halo.along_azimuth(sec_buf, ROW_HALO, NEAR, ROW_HALO, lanes)
        far[b] += halo.along_azimuth(ref_buf, REF_HALO, 0, REF_HALO, lanes)
    near_corners = halo.corners(sec_buf, ROW_HALO, 0, NEAR)
    far_corners = halo.corners(sec_buf, ROW_HALO, NEAR, ROW_HALO)
    far_corners += halo.corners(ref_buf, REF_HALO, 0, REF_HALO)

    halo.greet()
    halo.clear()
    for k in range(2):
        first = NEAR + off_az[k]
        at = lax.broadcasted_iota(jnp.int32, (384, 3 * REACH), 0)
        to = lax.broadcasted_iota(jnp.int32, (384, 3 * REACH), 1)
        at = at + (at // 128) * (REACH - 128)
        move = ones_where(to == at + first)
        for m in range(2):
            row_mats[k, m] = dot(sec_row_ref[k + m], move).astype(BF16)
        lag = lax.broadcasted_iota(jnp.int32, (64, 2 * REACH), 0)
        cell = lax.broadcasted_iota(jnp.int32, (64, 2 * REACH), 1)
        cell = jnp.where(cell < REACH, cell, cell - REACH) + (64 - 64 * k) - first - lag
        box_mid[k] = ones_where((cell >= 0) & (cell < CHIP))
        lag = lax.broadcasted_iota(jnp.int32, (64, 2 * FAR), 0)
        cell = lax.broadcasted_iota(jnp.int32, (64, 2 * FAR), 1)
        cell = jnp.where(cell < FAR, cell, cell - FAR) + REACH * k - first - lag
        box_far[k] = ones_where((cell >= 0) & (cell < CHIP))

    for load in halo.loads:
        load.wait()
    halo.meet()
    halo.start(near)
    halo.start(beside)
    for b in order:
        halo.start(far[b])

    own = pl.ds(LANE, COLS)
    ref_mean = jnp.mean(ref_buf[pl.ds(REF_HALO, ROWS), own], keepdims=True)
    sec_mean = jnp.mean(sec_buf[pl.ds(ROW_HALO, ROWS), own], keepdims=True)

    def reference_lines(m, pairs):
        parts = [ref_buf[64 * m : 64 * m + 64, LANE * p : LANE * p + 256] for p in pairs]
        parts = [shifted(x, LANE - REF_HALO, LANE) - ref_mean for x in parts]
        for p, x in zip(pairs, parts):
            place = pl.ds(LANE * p, LANE)
            stats[2 * m : 2 * m + 1, place] = jnp.sum(x, axis=0, keepdims=True)
            stats[2 * m + 1 : 2 * m + 2, place] = jnp.sum(x * x, axis=0, keepdims=True)
        high, low = split(jnp.concatenate(parts, axis=1))
        return dot(ref_row_ref[m], jnp.concatenate([high, low, high], axis=0))

    def window_lines(k, first, count, pairs, box_ref):
        parts = [sec_buf[first : first + count, LANE * p : LANE * p + 256] for p in pairs]
        parts = [shifted(x, 64 + off_rg[k], LANE) - sec_mean for x in parts]
        sums = []
        for p, x in zip(pairs, parts):
            high, low = split(x)
            square_high, square_low = split(x * x)
            place = pl.ds(LANE * p, LANE)
            sec_high[k, first : first + count, place] = high
            sec_low[k, first : first + count, place] = low
            stack = jnp.concatenate(
                [
                    jnp.concatenate([high, square_high], axis=1),
                    jnp.concatenate([low, square_low], axis=1),
                ],
                axis=0,
            )
            sums.append(dot(box_ref[k], stack))
        return sums

    def window_transform(k, m, pairs):
        rows = slice(64 * (k + m), 64 * (k + m) + REACH)
        high = jnp.concatenate([sec_high[k, rows, LANE * p : LANE * p + LANE] for p in pairs], axis=1)
        low = jnp.concatenate([sec_low[k, rows, LANE * p : LANE * p + LANE] for p in pairs], axis=1)
        return dot(row_mats[k, m], jnp.concatenate([high, low, high], axis=0))

    def store(target, pairs, blocks):
        for i, p in enumerate(pairs):
            for half in range(2):
                target[2 * p + half] = blocks[2 * i + half]

    def middle(pairs):
        rows_out = [reference_lines(1, pairs)]
        for k in range(2):
            for p, sums in zip(pairs, window_lines(k, 64, REACH, pairs, box_mid)):
                boxes[k, :64, pl.ds(LANE * p, LANE)] = sums[:, :128]
                boxes[k, 64:, pl.ds(LANE * p, LANE)] = sums[:, 128:]
            rows_out.append(window_transform(k, 1 - k, pairs))
        got = range_spectra(rows_out, col_ref)
        store(quads.at[1], pairs, got[0])
        store(windows.at[0, 1], pairs, got[1])
        store(windows.at[1, 0], pairs, got[2])

    def outer(pairs):
        for k in range(2):
            rows_out = [reference_lines(2 * k, pairs)]
            for p, sums in zip(pairs, window_lines(k, 224 * k, FAR, pairs, box_far)):
                boxes[k, :64, pl.ds(LANE * p, LANE)] += sums[:, :128]
                boxes[k, 64:, pl.ds(LANE * p, LANE)] += sums[:, 128:]
            rows_out.append(window_transform(k, k, pairs))
            got = range_spectra(rows_out, col_ref)
            store(quads.at[2 * k], pairs, got[0])
            store(windows.at[k, k], pairs, got[1])

    def strip(k, n):
        re, im = 0.0, 0.0
        for m in range(2):
            q = quads[k + m, n]
            x = windows[k, m, n] + windows[k, m, n + 1]
            qr, qi, xr, xi = q[:, :128], q[:, 128:], x[:, :128], x[:, 128:]
            re = re + (qr * xr + qi * xi)
            im = im + (qr * xi - qi * xr)
        return jnp.concatenate([re, im], axis=0)

    def finish(s):
        lane = s * LANE
        stat = stats[:, lane : lane + 256]
        place = lax.broadcasted_iota(jnp.int32, stat.shape, 1)
        a = jnp.sum(stat[:, :128], axis=1, keepdims=True)
        b = jnp.sum(jnp.where((place >= 64) & (place < 192), stat, 0.0), axis=1, keepdims=True)
        both = jnp.where(place[:, :128] < 64, a, b)
        for k in range(2):
            left, middle_, right = [strip(k, 2 * s + i) for i in range(3)]
            high, low = split(jnp.concatenate([left + middle_, middle_ + right], axis=1))
            y = dot(back_row_ref[:, :256], jnp.concatenate([high, low], axis=0))
            y = y + dot(back_row_ref[:, 256:], high)
            corr = 0.0
            for i in range(2):
                lanes = slice(LANE * i, LANE * i + LANE)
                high, low = split(jnp.concatenate([y[:64, lanes], y[64:, lanes]], axis=1))
                wide = dot(high, back_col_ref[i])
                corr = corr + (wide[:, :128] + wide[:, 128:]) + dot(low, back_col_ref[i, :, :128])
            high, low = split(boxes[k, :, lane : lane + 256])
            box = dot(high, box_col_ref[...]) + dot(low, box_col_ref[...])
            first, second = box[:64], box[64:]
            total = both[2 * k : 2 * k + 1] + both[2 * k + 2 : 2 * k + 3]
            power = both[2 * k + 1 : 2 * k + 2] + both[2 * k + 3 : 2 * k + 4]
            mean = total / AREA
            energy = power - total * mean
            centered = corr - mean * first
            var_sum = jnp.maximum(second - first * first / AREA, 0.0)
            score = (CHIP / AREA) * centered * lax.rsqrt((energy / AREA) * (var_sum / AREA) + EPSILON)
            high, low = split(score)
            lifted = dot(up_left_ref[...], jnp.concatenate([high, low], axis=0))
            high, low = split(lifted)
            wide = dot(high, up_right_ref[...]) + dot(low, up_right_ref[...])
            at = k * CHIPS + 2 * s
            staged[at] = wide[:, :128]
            staged[at + 1] = wide[:, 128:]
            pltpu.make_async_copy(staged.at[pl.ds(at, 2)], out_ref.at[pl.ds(at, 2)], sem).start()

    halo.arrive(near)
    halo.start(near_corners)
    middle((1, 2))
    middle((3, 4))
    halo.arrive(far[1] + far[6])
    halo.start(far_corners)
    middle((5,))
    halo.arrive(beside + near_corners)
    middle((0, 6))
    halo.arrive(far[2] + far[5])
    outer((1, 5))
    halo.arrive(far_corners)
    outer((0, 6))
    finish(0)
    finish(5)
    halo.arrive(far[3] + far[4])
    outer((2,))
    finish(1)
    outer((3, 4))
    finish(2)
    finish(3)
    finish(4)
    halo.close()
    pltpu.make_async_copy(staged, out_ref, sem).wait()


def body(ref_image, sec_image, off_az, off_rg):
    back_rows, back_cols = back_tables()
    left, right = cubic_tables()
    tables = [
        np.stack([azimuth_table(64 * m, 64) for m in range(3)]),
        np.stack([azimuth_table(64 * j, 128) for j in range(3)]),
        column_tables(),
        back_rows,
        back_cols,
        box_table(),
        left,
        right,
    ]
    vmem = pl.BlockSpec(memory_space=pltpu.VMEM)
    smem = pl.BlockSpec(memory_space=pltpu.SMEM)
    out = pl.pallas_call(
        kernel,
        out_shape=jax.ShapeDtypeStruct((2 * CHIPS, 128, 128), F32),
        in_specs=[smem, smem] + [pl.BlockSpec(memory_space=pl.ANY)] * 2 + [vmem] * len(tables),
        out_specs=pl.BlockSpec(memory_space=pl.ANY),
        scratch_shapes=[
            pltpu.VMEM((ROWS + 2 * REF_HALO, COLS + 2 * LANE), F32),
            pltpu.VMEM((ROWS + 2 * ROW_HALO, COLS + 2 * LANE), F32),
            pltpu.VMEM((2, 2, 128, 3 * REACH), BF16),
            pltpu.VMEM((2, 64, 2 * REACH), BF16),
            pltpu.VMEM((2, 64, 2 * FAR), BF16),
            pltpu.VMEM((2, ROWS + 2 * ROW_HALO, WIDE), BF16),
            pltpu.VMEM((2, ROWS + 2 * ROW_HALO, WIDE), BF16),
            pltpu.VMEM((3, BLOCKS, 64, 256), F32),
            pltpu.VMEM((2, 2, BLOCKS, 64, 256), F32),
            pltpu.VMEM((2, 128, WIDE), F32),
            pltpu.VMEM((8, WIDE), F32),
            pltpu.VMEM((2, 128, 128), F32),
            pltpu.VMEM((2 * CHIPS, 128, 128), F32),
            pltpu.SemaphoreType.DMA,
            pltpu.SemaphoreType.DMA((2,)),
            pltpu.SemaphoreType.DMA((48,)),
            pltpu.SemaphoreType.DMA((48,)),
        ],
        compiler_params=pltpu.CompilerParams(collective_id=0, has_side_effects=True),
    )(off_az, off_rg, ref_image, sec_image, *[jnp.asarray(t) for t in tables])
    return out.reshape(2, CHIPS, 128, 128)


def solution(mesh):
    return jax.shard_map(
        body,
        mesh=mesh,
        in_specs=(P("az", "rg"), P("az", "rg"), P("az"), P("az")),
        out_specs=P("az", "rg", None, None),
        check_vma=False,
    )
```

time: 53.2 us -> 27 us (0.51)
  starting transfers between devices: 27.7 us -> 0 us
  Pallas kernels: 15.5 us -> 24.1 us
  waiting for transfers between devices: 5.02 us -> 0 us
  other arithmetic: 2.15 us -> 0 us
    ppermute x8 -> x0, starting transfers between devices: 27.7 us -> none  [the longest x4 13.9 us: extended(): after = lax.ppermute(leading, axis, down)]
    pallas_call x1, Pallas kernels: 15.5 us -> 24.1 us  [body(): pl.pallas_call(kernel, out_shape=jax.ShapeDtypeStruct((2 * CHIPS, 128, 12...]
    ppermute x8 -> x0, waiting for transfers between devices: 5.02 us -> none  [the longest x4 3.52 us: extended(): after = lax.ppermute(leading, axis, down)]
    unnamed x8 -> x1, local copies, waits for them, and re-layouts: 0.09 us -> 2.7 us
    concatenate x2 -> x0, other arithmetic: 2.15 us -> none  [extended(): value = jnp.concatenate([before, value, after], axis=dim)]
    slice x4 -> x0, local copies, waits for them, and re-layouts: 2.14 us -> none  [the longest x2 2.1 us: extended(): leading = lax.slice_in_dim(value, 0, width, axis=dim)]
  transfers between devices with their start and end apart: 8 -> 0, of which waited for: 2 -> 0; matrix products, arithmetic and copies ran while one was open for 4% -> 0% of each run, Pallas kernels for 0% -> 0%
where the time goes in v2:
time: 27 us; the launch traced here: 26.8 us
  Pallas kernels  24.1 us (89%)
  local copies, waits for them, and re-layouts  2.7 us (10%)
    pallas_call x1, Pallas kernels, body(): pl.pallas_call(kernel, out_shape=jax.ShapeDtypeStruct((2 * CHIPS, 128, 12...  24.1 us
    unnamed x1, local copies, waits for them, and re-layouts  2.7 us

profile of v2, /device:TPU:99, one launch (start us, length us, event | category | flops | bytes accessed | tf_op | source)
XLA Modules:
  0.0 26.8 jit_solution(7359263112775687599)
XLA Ops:
  0.0 24.1 %shard_map.118 = f32[24,128,128]{2,1,0:T(8,128)} custom-call(s32[2]{0:T(128)} %off_az.1, s32[2]{0:T(128)} %off_rg.1, f32[128,768]{1,0:T(8,128)} %ref_tile.1, f32[128,768]{1,0:T(8,128)} %sec_tile.1, bf16[3,128,192]{2,1,0:T(8,128)(2,1)} %constant.16.clone.ref_row_ref, bf16[3,128,384]{2,1,0:T(8,128)(2,1)} %constant.17.clone.sec_row_ref, ...), custom_call_target="tpu_custom_call" | custom-call | tf_op jit(solution)/shard_map/pallas_call | solution.py:486
  24.1 2.7 %copy.14 = f32[2,12,128,128]{3,2,1,0:T(8,128)} copy(f32[2,12,128,128]{3,2,1,0:T(8,128)} %bitcast.1) | data formatting | bytes 3145728

commit v3 on v2

--- a/solution.py
+++ b/solution.py
@@ -248,38 +248,11 @@
                 transfer.wait_send()
 
 
-def kernel(
-    off_az,
-    off_rg,
-    ref_tile,
-    sec_tile,
-    ref_row_ref,
-    sec_row_ref,
-    col_ref,
-    back_row_ref,
-    back_col_ref,
-    box_col_ref,
-    up_left_ref,
-    up_right_ref,
-    out_ref,
-    ref_buf,
-    sec_buf,
-    row_mats,
-    box_mid,
-    box_far,
-    sec_high,
-    sec_low,
-    quads,
-    windows,
-    boxes,
-    stats,
-    strips,
-    staged,
-    sem,
-    tile_sems,
-    send_sems,
-    recv_sems,
-):
+def kernel(off_az, off_rg, ref_tile, sec_tile, *refs):
+    table_hbm, out_ref, tables = refs[:8], refs[8], refs[9:17]
+    ref_row_ref, sec_row_ref, col_ref, back_row_ref, back_col_ref, box_col_ref, up_left_ref, up_right_ref = tables
+    ref_buf, sec_buf, row_mats, box_mid, box_far, sec_high, sec_low, square_high, square_low = refs[17:26]
+    quads, windows, boxes, stats, staged, sem, tile_sems, table_sems, send_sems, recv_sems = refs[26:]
     halo = Exchange(
         (ref_tile, sec_tile),
         ((ref_buf, REF_HALO), (sec_buf, ROW_HALO)),
@@ -301,15 +274,37 @@
     far_corners += halo.corners(ref_buf, REF_HALO, 0, REF_HALO)
 
     halo.greet()
+    fetches = [
+        pltpu.make_async_copy(source, target, table_sems.at[i])
+        for i, (source, target) in enumerate(zip(table_hbm, tables))
+    ]
+    for fetch in fetches:
+        fetch.start()
     halo.clear()
+    for load in halo.loads:
+        load.wait()
+    halo.meet()
+    halo.start(near)
+    halo.start(beside)
+    for b in order:
+        halo.start(far[b])
+
+    own = pl.ds(LANE, COLS)
+    ref_mean = jnp.mean(ref_buf[pl.ds(REF_HALO, ROWS), own], keepdims=True)
+    sec_mean = jnp.mean(sec_buf[pl.ds(ROW_HALO, ROWS), own], keepdims=True)
+
+    for fetch in fetches:
+        fetch.wait()
+    lane = lax.broadcasted_iota(jnp.int32, (128, LANE), 1)
     for k in range(2):
         first = NEAR + off_az[k]
-        at = lax.broadcasted_iota(jnp.int32, (384, 3 * REACH), 0)
-        to = lax.broadcasted_iota(jnp.int32, (384, 3 * REACH), 1)
-        at = at + (at // 128) * (REACH - 128)
-        move = ones_where(to == at + first)
         for m in range(2):
-            row_mats[k, m] = dot(sec_row_ref[k + m], move).astype(BF16)
+            turned = [
+                pltpu.roll(sec_row_ref[k + m, :, i : i + LANE], first, axis=1)
+                for i in range(0, 512, LANE)
+            ]
+            moved = [jnp.where(lane < first, turned[i - 1], turned[i]) for i in range(4)]
+            row_mats[k, m] = jnp.concatenate(moved, axis=1)[:, : 3 * REACH].astype(BF16)
         lag = lax.broadcasted_iota(jnp.int32, (64, 2 * REACH), 0)
         cell = lax.broadcasted_iota(jnp.int32, (64, 2 * REACH), 1)
         cell = jnp.where(cell < REACH, cell, cell - REACH) + (64 - 64 * k) - first - lag
@@ -318,18 +313,6 @@
         cell = lax.broadcasted_iota(jnp.int32, (64, 2 * FAR), 1)
         cell = jnp.where(cell < FAR, cell, cell - FAR) + REACH * k - first - lag
         box_far[k] = ones_where((cell >= 0) & (cell < CHIP))
-
-    for load in halo.loads:
-        load.wait()
-    halo.meet()
-    halo.start(near)
-    halo.start(beside)
-    for b in order:
-        halo.start(far[b])
-
-    own = pl.ds(LANE, COLS)
-    ref_mean = jnp.mean(ref_buf[pl.ds(REF_HALO, ROWS), own], keepdims=True)
-    sec_mean = jnp.mean(sec_buf[pl.ds(ROW_HALO, ROWS), own], keepdims=True)
 
     def reference_lines(m, pairs):
         parts = [ref_buf[64 * m : 64 * m + 64, LANE * p : LANE * p + 256] for p in pairs]
@@ -341,25 +324,25 @@
         high, low = split(jnp.concatenate(parts, axis=1))
         return dot(ref_row_ref[m], jnp.concatenate([high, low, high], axis=0))
 
-    def window_lines(k, first, count, pairs, box_ref):
-        parts = [sec_buf[first : first + count, LANE * p : LANE * p + 256] for p in pairs]
-        parts = [shifted(x, 64 + off_rg[k], LANE) - sec_mean for x in parts]
-        sums = []
-        for p, x in zip(pairs, parts):
-            high, low = split(x)
-            square_high, square_low = split(x * x)
-            place = pl.ds(LANE * p, LANE)
-            sec_high[k, first : first + count, place] = high
-            sec_low[k, first : first + count, place] = low
-            stack = jnp.concatenate(
-                [
-                    jnp.concatenate([high, square_high], axis=1),
-                    jnp.concatenate([low, square_low], axis=1),
-                ],
-                axis=0,
-            )
-            sums.append(dot(box_ref[k], stack))
-        return sums
+    def take_lines(k, spans, pairs):
+        for p in pairs:
+            place = slice(LANE * p, LANE * p + LANE)
+            for first, count in spans:
+                rows = slice(first, first + count)
+                x = shifted(sec_buf[rows, LANE * p : LANE * p + 256], 64 + off_rg[k], LANE) - sec_mean
+                sec_high[k, rows, place], sec_low[k, rows, place] = split(x)
+                square_high[k, rows, place], square_low[k, rows, place] = split(x * x)
+
+    def box_lines(k, first, count, p, box_ref):
+        rows, place = slice(first, first + count), slice(LANE * p, LANE * p + LANE)
+        stack = jnp.concatenate(
+            [
+                jnp.concatenate([sec_high[k, rows, place], square_high[k, rows, place]], axis=1),
+                jnp.concatenate([sec_low[k, rows, place], square_low[k, rows, place]], axis=1),
+            ],
+            axis=0,
+        )
+        return dot(box_ref[k], stack)
 
     def window_transform(k, m, pairs):
         rows = slice(64 * (k + m), 64 * (k + m) + REACH)
@@ -372,28 +355,46 @@
             for half in range(2):
                 target[2 * p + half] = blocks[2 * i + half]
 
-    def middle(pairs):
-        rows_out = [reference_lines(1, pairs)]
-        for k in range(2):
-            for p, sums in zip(pairs, window_lines(k, 64, REACH, pairs, box_mid)):
-                boxes[k, :64, pl.ds(LANE * p, LANE)] = sums[:, :128]
-                boxes[k, 64:, pl.ds(LANE * p, LANE)] = sums[:, 128:]
-            rows_out.append(window_transform(k, 1 - k, pairs))
-        got = range_spectra(rows_out, col_ref)
-        store(quads.at[1], pairs, got[0])
-        store(windows.at[0, 1], pairs, got[1])
-        store(windows.at[1, 0], pairs, got[2])
-
-    def outer(pairs):
-        for k in range(2):
-            rows_out = [reference_lines(2 * k, pairs)]
-            for p, sums in zip(pairs, window_lines(k, 224 * k, FAR, pairs, box_far)):
-                boxes[k, :64, pl.ds(LANE * p, LANE)] += sums[:, :128]
-                boxes[k, 64:, pl.ds(LANE * p, LANE)] += sums[:, 128:]
-            rows_out.append(window_transform(k, k, pairs))
-            got = range_spectra(rows_out, col_ref)
-            store(quads.at[2 * k], pairs, got[0])
-            store(windows.at[k, k], pairs, got[1])
+    def middle_quadrants(*groups):
+        rows_out = [reference_lines(1, pairs) for pairs in groups]
+        for pairs, x in zip(groups, rows_out):
+            store(quads.at[1], pairs, range_spectra([x], col_ref)[0])
+
+    def middle_windows(*groups):
+        rows_out = [[window_transform(k, 1 - k, pairs) for k in range(2)] for pairs in groups]
+        for pairs in groups:
+            for k in range(2):
+                for p in pairs:
+                    sums = box_lines(k, 64, REACH, p, box_mid)
+                    boxes[k, :64, LANE * p : LANE * p + LANE] = sums[:, :128]
+                    boxes[k, 64:, LANE * p : LANE * p + LANE] = sums[:, 128:]
+        for pairs, x in zip(groups, rows_out):
+            got = range_spectra(x, col_ref)
+            store(windows.at[0, 1], pairs, got[0])
+            store(windows.at[1, 0], pairs, got[1])
+
+    def outer(*groups):
+        for pairs in groups:
+            take_lines(0, ((0, FAR),), pairs)
+            take_lines(1, ((224, FAR),), pairs)
+        rows_out = [
+            [
+                [reference_lines(2 * k, pairs), window_transform(k, k, pairs)]
+                for k in range(2)
+            ]
+            for pairs in groups
+        ]
+        for pairs in groups:
+            for k in range(2):
+                for p in pairs:
+                    sums = box_lines(k, 224 * k, FAR, p, box_far)
+                    boxes[k, :64, LANE * p : LANE * p + LANE] += sums[:, :128]
+                    boxes[k, 64:, LANE * p : LANE * p + LANE] += sums[:, 128:]
+        for pairs, x in zip(groups, rows_out):
+            for k in range(2):
+                got = range_spectra(x[k], col_ref)
+                store(quads.at[2 * k], pairs, got[0])
+                store(windows.at[k, k], pairs, got[1])
 
     def strip(k, n):
         re, im = 0.0, 0.0
@@ -405,67 +406,96 @@
             im = im + (qr * xi - qi * xr)
         return jnp.concatenate([re, im], axis=0)
 
-    def finish(s):
-        lane = s * LANE
-        stat = stats[:, lane : lane + 256]
-        place = lax.broadcasted_iota(jnp.int32, stat.shape, 1)
-        a = jnp.sum(stat[:, :128], axis=1, keepdims=True)
-        b = jnp.sum(jnp.where((place >= 64) & (place < 192), stat, 0.0), axis=1, keepdims=True)
-        both = jnp.where(place[:, :128] < 64, a, b)
-        for k in range(2):
-            left, middle_, right = [strip(k, 2 * s + i) for i in range(3)]
+    def finish(*pairs):
+        items = [(k, s) for s in pairs for k in range(2)]
+        moments = {}
+        for s in pairs:
+            stat = stats[:, s * LANE : s * LANE + 256]
+            place = lax.broadcasted_iota(jnp.int32, stat.shape, 1)
+            a = jnp.sum(stat[:, :128], axis=1, keepdims=True)
+            b = jnp.sum(jnp.where((place >= 64) & (place < 192), stat, 0.0), axis=1, keepdims=True)
+            moments[s] = jnp.where(place[:, :128] < 64, a, b)
+        sums = {}
+        for k, s in items:
+            for n in range(2 * s, 2 * s + 3):
+                if (k, n) not in sums:
+                    sums[k, n] = strip(k, n)
+        inner = {}
+        for k, s in items:
+            left, middle_, right = [sums[k, 2 * s + i] for i in range(3)]
             high, low = split(jnp.concatenate([left + middle_, middle_ + right], axis=1))
             y = dot(back_row_ref[:, :256], jnp.concatenate([high, low], axis=0))
-            y = y + dot(back_row_ref[:, 256:], high)
+            inner[k, s] = y + dot(back_row_ref[:, 256:], high)
+        scores = {}
+        for k, s in items:
+            y = inner[k, s]
             corr = 0.0
             for i in range(2):
                 lanes = slice(LANE * i, LANE * i + LANE)
                 high, low = split(jnp.concatenate([y[:64, lanes], y[64:, lanes]], axis=1))
                 wide = dot(high, back_col_ref[i])
                 corr = corr + (wide[:, :128] + wide[:, 128:]) + dot(low, back_col_ref[i, :, :128])
-            high, low = split(boxes[k, :, lane : lane + 256])
+            high, low = split(boxes[k, :, s * LANE : s * LANE + 256])
             box = dot(high, box_col_ref[...]) + dot(low, box_col_ref[...])
             first, second = box[:64], box[64:]
+            both = moments[s]
             total = both[2 * k : 2 * k + 1] + both[2 * k + 2 : 2 * k + 3]
             power = both[2 * k + 1 : 2 * k + 2] + both[2 * k + 3 : 2 * k + 4]
             mean = total / AREA
             energy = power - total * mean
             centered = corr - mean * first
             var_sum = jnp.maximum(second - first * first / AREA, 0.0)
-            score = (CHIP / AREA) * centered * lax.rsqrt((energy / AREA) * (var_sum / AREA) + EPSILON)
-            high, low = split(score)
-            lifted = dot(up_left_ref[...], jnp.concatenate([high, low], axis=0))
-            high, low = split(lifted)
+            scores[k, s] = (CHIP / AREA) * centered * lax.rsqrt(
+                (energy / AREA) * (var_sum / AREA) + EPSILON
+            )
+        lifted = {}
+        for k, s in items:
+            high, low = split(scores[k, s])
+            lifted[k, s] = dot(up_left_ref[...], jnp.concatenate([high, low], axis=0))
+        for k, s in items:
+            high, low = split(lifted[k, s])
             wide = dot(high, up_right_ref[...]) + dot(low, up_right_ref[...])
             at = k * CHIPS + 2 * s
             staged[at] = wide[:, :128]
             staged[at + 1] = wide[:, 128:]
+        for k, s in items:
+            at = k * CHIPS + 2 * s
             pltpu.make_async_copy(staged.at[pl.ds(at, 2)], out_ref.at[pl.ds(at, 2)], sem).start()
 
+    inside = (1, 2, 3, 4, 5)
+    near_lines = ((ROW_HALO - NEAR, NEAR), (ROW_HALO + ROWS, NEAR))
+    middle_quadrants((1, 2), (3, 4), (5,))
+    for k in range(2):
+        take_lines(k, ((ROW_HALO, ROWS),), inside)
     halo.arrive(near)
     halo.start(near_corners)
-    middle((1, 2))
-    middle((3, 4))
+    for k in range(2):
+        take_lines(k, near_lines, inside)
+    middle_windows((1, 2), (3, 4), (5,))
     halo.arrive(far[1] + far[6])
     halo.start(far_corners)
-    middle((5,))
-    halo.arrive(beside + near_corners)
-    middle((0, 6))
+    halo.arrive(beside)
+    middle_quadrants((0, 6))
+    halo.arrive(near_corners)
+    for k in range(2):
+        take_lines(k, near_lines + ((ROW_HALO, ROWS),), (0, 6))
+    middle_windows((0, 6))
     halo.arrive(far[2] + far[5])
     outer((1, 5))
     halo.arrive(far_corners)
     outer((0, 6))
-    finish(0)
-    finish(5)
+    finish(0, 5)
     halo.arrive(far[3] + far[4])
-    outer((2,))
-    finish(1)
-    outer((3, 4))
-    finish(2)
-    finish(3)
-    finish(4)
+    outer((2,), (3, 4))
+    finish(1, 2, 3, 4)
     halo.close()
     pltpu.make_async_copy(staged, out_ref, sem).wait()
+
+
+def spread(table):
+    room = np.zeros((128, REACH - 128))
+    parts = [np.concatenate([table[:, i : i + 128].astype(np.float64), room], 1) for i in (0, 128, 256)]
+    return np.concatenate(parts + [room], axis=1).astype(np.float32)
 
 
 def body(ref_image, sec_image, off_az, off_rg):
@@ -473,7 +503,7 @@
     left, right = cubic_tables()
     tables = [
         np.stack([azimuth_table(64 * m, 64) for m in range(3)]),
-        np.stack([azimuth_table(64 * j, 128) for j in range(3)]),
+        np.stack([spread(azimuth_table(64 * j, 128)) for j in range(3)]),
         column_tables(),
         back_rows,
         back_cols,
@@ -481,14 +511,14 @@
         left,
         right,
     ]
-    vmem = pl.BlockSpec(memory_space=pltpu.VMEM)
     smem = pl.BlockSpec(memory_space=pltpu.SMEM)
     out = pl.pallas_call(
         kernel,
         out_shape=jax.ShapeDtypeStruct((2 * CHIPS, 128, 128), F32),
-        in_specs=[smem, smem] + [pl.BlockSpec(memory_space=pl.ANY)] * 2 + [vmem] * len(tables),
+        in_specs=[smem, smem] + [pl.BlockSpec(memory_space=pl.ANY)] * (2 + len(tables)),
         out_specs=pl.BlockSpec(memory_space=pl.ANY),
-        scratch_shapes=[
+        scratch_shapes=[pltpu.VMEM(t.shape, t.dtype) for t in tables]
+        + [
             pltpu.VMEM((ROWS + 2 * REF_HALO, COLS + 2 * LANE), F32),
             pltpu.VMEM((ROWS + 2 * ROW_HALO, COLS + 2 * LANE), F32),
             pltpu.VMEM((2, 2, 128, 3 * REACH), BF16),
@@ -496,14 +526,16 @@
             pltpu.VMEM((2, 64, 2 * FAR), BF16),
             pltpu.VMEM((2, ROWS + 2 * ROW_HALO, WIDE), BF16),
             pltpu.VMEM((2, ROWS + 2 * ROW_HALO, WIDE), BF16),
+            pltpu.VMEM((2, ROWS + 2 * ROW_HALO, WIDE), BF16),
+            pltpu.VMEM((2, ROWS + 2 * ROW_HALO, WIDE), BF16),
             pltpu.VMEM((3, BLOCKS, 64, 256), F32),
             pltpu.VMEM((2, 2, BLOCKS, 64, 256), F32),
             pltpu.VMEM((2, 128, WIDE), F32),
             pltpu.VMEM((8, WIDE), F32),
-            pltpu.VMEM((2, 128, 128), F32),
             pltpu.VMEM((2 * CHIPS, 128, 128), F32),
             pltpu.SemaphoreType.DMA,
             pltpu.SemaphoreType.DMA((2,)),
+            pltpu.SemaphoreType.DMA((8,)),
             pltpu.SemaphoreType.DMA((48,)),
             pltpu.SemaphoreType.DMA((48,)),
         ],

time: 27 us -> 23 us (0.85)
  Pallas kernels: 24.1 us -> 20.1 us
    pallas_call x1, Pallas kernels: 24.1 us -> 20.1 us  [body(): pl.pallas_call(kernel, out_shape=jax.ShapeDtypeStruct((2 * CHIPS, 128, 12...]
where the time goes in v3:
time: 23 us; the launch traced here: 22.8 us
  Pallas kernels  20.1 us (87%)
  local copies, waits for them, and re-layouts  2.7 us (12%)
    pallas_call x1, Pallas kernels, body(): pl.pallas_call(kernel, out_shape=jax.ShapeDtypeStruct((2 * CHIPS, 128, 12...  20.1 us
    unnamed x1, local copies, waits for them, and re-layouts  2.7 us

profile of v3, /device:TPU:99, one launch (start us, length us, event | category | flops | bytes accessed | tf_op | source)
XLA Modules:
  0.0 22.8 jit_solution(1329677704528874050)
XLA Ops:
  0.0 20.1 %shard_map.118 = f32[24,128,128]{2,1,0:T(8,128)} custom-call(s32[2]{0:T(128)} %off_az.1, s32[2]{0:T(128)} %off_rg.1, f32[128,768]{1,0:T(8,128)} %ref_tile.1, f32[128,768]{1,0:T(8,128)} %sec_tile.1, bf16[3,128,192]{2,1,0:T(8,128)(2,1)} %constant.16.clone.refs_0_, f32[3,128,512]{2,1,0:T(8,128)} %constant.17.clone.refs_1_, ...), custom_call_target="tpu_custom_call" | custom-call | tf_op jit(solution)/shard_map/pallas_call | solution.py:515
  20.1 2.7 %copy.14 = f32[2,12,128,128]{3,2,1,0:T(8,128)} copy(f32[2,12,128,128]{3,2,1,0:T(8,128)} %bitcast.1) | data formatting | bytes 3145728

commit v4 on v3

--- a/solution.py
+++ b/solution.py
@@ -72,20 +72,6 @@
     first = np.concatenate([high, none, low, none], axis=1)
     second = np.concatenate([none, high, none, low], axis=1)
     return rows, np.stack([first, second])
-
-
-def cubic_tables():
-    table = np.zeros((128, 64))
-    for m in range(64):
-        table[2 * m, m] = 1.0
-        for step, weight in ((0, 9.0), (1, 9.0), (-1, -1.0), (2, -1.0)):
-            table[2 * m + 1, min(max(m + step, 0), 63)] += weight / 16.0
-    left = np.concatenate([table, table], axis=1)
-    none = np.zeros((64, 128))
-    right = np.concatenate(
-        [np.concatenate([table.T, none], 1), np.concatenate([none, table.T], 1)], axis=0
-    )
-    return left.astype(jnp.bfloat16), right.astype(jnp.bfloat16)
 
 
 def split(x):
@@ -248,11 +234,12 @@
                 transfer.wait_send()
 
 
-def kernel(off_az, off_rg, ref_tile, sec_tile, *refs):
-    table_hbm, out_ref, tables = refs[:8], refs[8], refs[9:17]
-    ref_row_ref, sec_row_ref, col_ref, back_row_ref, back_col_ref, box_col_ref, up_left_ref, up_right_ref = tables
-    ref_buf, sec_buf, row_mats, box_mid, box_far, sec_high, sec_low, square_high, square_low = refs[17:26]
-    quads, windows, boxes, stats, staged, sem, tile_sems, table_sems, send_sems, recv_sems = refs[26:]
+def kernel(off_az_hbm, off_rg_hbm, ref_tile, sec_tile, *refs):
+    table_hbm, score_ref, tables = refs[:6], refs[6], refs[7:13]
+    ref_row_ref, sec_row_ref, col_ref, back_row_ref, back_col_ref, box_col_ref = tables
+    off_az, off_rg, ref_buf, sec_buf, row_mats, box_mid, box_far = refs[13:20]
+    sec_high, sec_low, square_high, square_low = refs[20:24]
+    quads, windows, strips, boxes, stats, tile_sems, table_sems, send_sems, recv_sems = refs[24:]
     halo = Exchange(
         (ref_tile, sec_tile),
         ((ref_buf, REF_HALO), (sec_buf, ROW_HALO)),
@@ -263,20 +250,22 @@
     everything = (LANE, COLS)
     near = halo.along_azimuth(sec_buf, ROW_HALO, 0, NEAR, everything)
     beside = halo.along_range(sec_buf, (ROW_HALO, ROWS)) + halo.along_range(ref_buf, (REF_HALO, ROWS))
-    far = {}
     order = (1, 6, 2, 5, 3, 4)
+    sec_far, ref_far = {}, {}
     for b in order:
-        lanes = (LANE * b, LANE)
-        far[b] = halo.along_azimuth(sec_buf, ROW_HALO, NEAR, ROW_HALO, lanes)
-        far[b] += halo.along_azimuth(ref_buf, REF_HALO, 0, REF_HALO, lanes)
+        sec_far[b] = halo.along_azimuth(sec_buf, ROW_HALO, NEAR, ROW_HALO, (LANE * b, LANE))
+    for b, lanes in ((1, (LANE, LANE)), (6, (COLS, LANE)), (2, (2 * LANE, 4 * LANE))):
+        ref_far[b] = halo.along_azimuth(ref_buf, REF_HALO, 0, REF_HALO, lanes)
     near_corners = halo.corners(sec_buf, ROW_HALO, 0, NEAR)
-    far_corners = halo.corners(sec_buf, ROW_HALO, NEAR, ROW_HALO)
-    far_corners += halo.corners(ref_buf, REF_HALO, 0, REF_HALO)
+    sec_corners = halo.corners(sec_buf, ROW_HALO, NEAR, ROW_HALO)
+    ref_corners = halo.corners(ref_buf, REF_HALO, 0, REF_HALO)
 
     halo.greet()
     fetches = [
         pltpu.make_async_copy(source, target, table_sems.at[i])
-        for i, (source, target) in enumerate(zip(table_hbm, tables))
+        for i, (source, target) in enumerate(
+            zip((off_az_hbm, off_rg_hbm) + table_hbm, (off_az, off_rg) + tables)
+        )
     ]
     for fetch in fetches:
         fetch.start()
@@ -286,8 +275,10 @@
     halo.meet()
     halo.start(near)
     halo.start(beside)
-    for b in order:
-        halo.start(far[b])
+    halo.start(sec_far[1] + sec_far[6])
+    halo.start(ref_far[1] + ref_far[6] + ref_far[2])
+    for b in order[2:]:
+        halo.start(sec_far[b])
 
     own = pl.ds(LANE, COLS)
     ref_mean = jnp.mean(ref_buf[pl.ds(REF_HALO, ROWS), own], keepdims=True)
@@ -373,17 +364,18 @@
             store(windows.at[0, 1], pairs, got[0])
             store(windows.at[1, 0], pairs, got[1])
 
-    def outer(*groups):
+    def outer_quadrants(*groups):
+        rows_out = [[reference_lines(m, pairs) for m in (0, 2)] for pairs in groups]
+        for pairs, x in zip(groups, rows_out):
+            got = range_spectra(x, col_ref)
+            store(quads.at[0], pairs, got[0])
+            store(quads.at[2], pairs, got[1])
+
+    def outer_windows(*groups):
         for pairs in groups:
             take_lines(0, ((0, FAR),), pairs)
             take_lines(1, ((224, FAR),), pairs)
-        rows_out = [
-            [
-                [reference_lines(2 * k, pairs), window_transform(k, k, pairs)]
-                for k in range(2)
-            ]
-            for pairs in groups
-        ]
+        rows_out = [[window_transform(k, k, pairs) for k in range(2)] for pairs in groups]
         for pairs in groups:
             for k in range(2):
                 for p in pairs:
@@ -391,20 +383,28 @@
                     boxes[k, :64, LANE * p : LANE * p + LANE] += sums[:, :128]
                     boxes[k, 64:, LANE * p : LANE * p + LANE] += sums[:, 128:]
         for pairs, x in zip(groups, rows_out):
+            got = range_spectra(x, col_ref)
             for k in range(2):
-                got = range_spectra(x[k], col_ref)
-                store(quads.at[2 * k], pairs, got[0])
-                store(windows.at[k, k], pairs, got[1])
+                store(windows.at[k, k], pairs, got[k])
+
+    def product(k, m, n):
+        q = quads[k + m, n]
+        x = windows[k, m, n] + windows[k, m, n + 1]
+        qr, qi, xr, xi = q[:, :128], q[:, 128:], x[:, :128], x[:, 128:]
+        return jnp.concatenate([qr * xr + qi * xi, qr * xi - qi * xr], axis=0)
+
+    def middle_strips(*numbers):
+        for n in numbers:
+            for k in range(2):
+                strips[k, n] = product(k, 1 - k, n)
+
+    done = {}
 
     def strip(k, n):
-        re, im = 0.0, 0.0
-        for m in range(2):
-            q = quads[k + m, n]
-            x = windows[k, m, n] + windows[k, m, n + 1]
-            qr, qi, xr, xi = q[:, :128], q[:, 128:], x[:, :128], x[:, 128:]
-            re = re + (qr * xr + qi * xi)
-            im = im + (qr * xi - qi * xr)
-        return jnp.concatenate([re, im], axis=0)
+        if (k, n) not in done:
+            done[k, n] = True
+            strips[k, n] += product(k, k, n)
+        return strips[k, n]
 
     def finish(*pairs):
         items = [(k, s) for s in pairs for k in range(2)]
@@ -415,18 +415,13 @@
             a = jnp.sum(stat[:, :128], axis=1, keepdims=True)
             b = jnp.sum(jnp.where((place >= 64) & (place < 192), stat, 0.0), axis=1, keepdims=True)
             moments[s] = jnp.where(place[:, :128] < 64, a, b)
-        sums = {}
-        for k, s in items:
-            for n in range(2 * s, 2 * s + 3):
-                if (k, n) not in sums:
-                    sums[k, n] = strip(k, n)
+        sums = {(k, n): strip(k, n) for k, s in items for n in range(2 * s, 2 * s + 3)}
         inner = {}
         for k, s in items:
             left, middle_, right = [sums[k, 2 * s + i] for i in range(3)]
             high, low = split(jnp.concatenate([left + middle_, middle_ + right], axis=1))
             y = dot(back_row_ref[:, :256], jnp.concatenate([high, low], axis=0))
             inner[k, s] = y + dot(back_row_ref[:, 256:], high)
-        scores = {}
         for k, s in items:
             y = inner[k, s]
             corr = 0.0
@@ -445,22 +440,9 @@
             energy = power - total * mean
             centered = corr - mean * first
             var_sum = jnp.maximum(second - first * first / AREA, 0.0)
-            scores[k, s] = (CHIP / AREA) * centered * lax.rsqrt(
+            score_ref[k, s] = (CHIP / AREA) * centered * lax.rsqrt(
                 (energy / AREA) * (var_sum / AREA) + EPSILON
             )
-        lifted = {}
-        for k, s in items:
-            high, low = split(scores[k, s])
-            lifted[k, s] = dot(up_left_ref[...], jnp.concatenate([high, low], axis=0))
-        for k, s in items:
-            high, low = split(lifted[k, s])
-            wide = dot(high, up_right_ref[...]) + dot(low, up_right_ref[...])
-            at = k * CHIPS + 2 * s
-            staged[at] = wide[:, :128]
-            staged[at + 1] = wide[:, 128:]
-        for k, s in items:
-            at = k * CHIPS + 2 * s
-            pltpu.make_async_copy(staged.at[pl.ds(at, 2)], out_ref.at[pl.ds(at, 2)], sem).start()
 
     inside = (1, 2, 3, 4, 5)
     near_lines = ((ROW_HALO - NEAR, NEAR), (ROW_HALO + ROWS, NEAR))
@@ -472,23 +454,64 @@
     for k in range(2):
         take_lines(k, near_lines, inside)
     middle_windows((1, 2), (3, 4), (5,))
-    halo.arrive(far[1] + far[6])
-    halo.start(far_corners)
+    halo.arrive(sec_far[1] + sec_far[6])
+    halo.start(sec_corners)
     halo.arrive(beside)
     middle_quadrants((0, 6))
+    halo.arrive(ref_far[1] + ref_far[6])
+    halo.start(ref_corners)
     halo.arrive(near_corners)
     for k in range(2):
         take_lines(k, near_lines + ((ROW_HALO, ROWS),), (0, 6))
     middle_windows((0, 6))
-    halo.arrive(far[2] + far[5])
-    outer((1, 5))
-    halo.arrive(far_corners)
-    outer((0, 6))
-    finish(0, 5)
-    halo.arrive(far[3] + far[4])
-    outer((2,), (3, 4))
-    finish(1, 2, 3, 4)
+    middle_strips(*range(BLOCKS - 1))
+    halo.arrive(ref_far[2])
+    outer_quadrants((1, 2), (3, 4), (5,))
+    halo.arrive(ref_corners)
+    outer_quadrants((0, 6))
+    halo.arrive(sec_far[2] + sec_far[5] + sec_corners)
+    outer_windows((1, 5), (0, 6))
+    halo.arrive(sec_far[3])
+    outer_windows((2,))
+    finish(0, 1, 5)
+    halo.arrive(sec_far[4])
+    outer_windows((3, 4))
+    finish(2, 3, 4)
     halo.close()
+
+
+def oversample(score_ref, out_ref, staged, sem):
+    def cubic(out_index, sample):
+        base = out_index // 2
+
+        def pick(step):
+            return jnp.where(jnp.clip(base + step, 0, LAGS - 1) == sample, 1.0, 0.0)
+
+        odd = (9.0 * (pick(0) + pick(1)) - (pick(-1) + pick(2))) / 16.0
+        return jnp.where(out_index % 2 == 1, odd, pick(0))
+
+    row = lax.broadcasted_iota(jnp.int32, (128, 128), 0)
+    lane = lax.broadcasted_iota(jnp.int32, (128, 128), 1)
+    left = cubic(row, lane % LAGS).astype(BF16)
+    right = cubic(lane, row % LAGS)
+    right = jnp.concatenate(
+        [jnp.where(row < LAGS, right, 0.0), jnp.where(row < LAGS, 0.0, right)], axis=1
+    ).astype(BF16)
+    items = [(k, s) for k in range(2) for s in range(PAIRS)]
+    for some in (items[:4], items[4:8], items[8:]):
+        lifted = []
+        for k, s in some:
+            high, low = split(score_ref[k, s])
+            lifted.append(dot(left, jnp.concatenate([high, low], axis=0)))
+        for (k, s), value in zip(some, lifted):
+            high, low = split(value)
+            wide = dot(high, right) + dot(low, right)
+            at = k * CHIPS + 2 * s
+            staged[at] = wide[:, :128]
+            staged[at + 1] = wide[:, 128:]
+        for k, s in some:
+            part = pl.ds(k * CHIPS + 2 * s, 2)
+            pltpu.make_async_copy(staged.at[part], out_ref.at[part], sem).start()
     pltpu.make_async_copy(staged, out_ref, sem).wait()
 
 
@@ -500,7 +523,6 @@
 
 def body(ref_image, sec_image, off_az, off_rg):
     back_rows, back_cols = back_tables()
-    left, right = cubic_tables()
     tables = [
         np.stack([azimuth_table(64 * m, 64) for m in range(3)]),
         np.stack([spread(azimuth_table(64 * j, 128)) for j in range(3)]),
@@ -508,39 +530,48 @@
         back_rows,
         back_cols,
         box_table(),
-        left,
-        right,
     ]
-    smem = pl.BlockSpec(memory_space=pltpu.SMEM)
-    out = pl.pallas_call(
+    anywhere = pl.BlockSpec(memory_space=pl.ANY)
+    vmem = pl.BlockSpec(memory_space=pltpu.VMEM)
+    scores = pl.pallas_call(
         kernel,
-        out_shape=jax.ShapeDtypeStruct((2 * CHIPS, 128, 128), F32),
-        in_specs=[smem, smem] + [pl.BlockSpec(memory_space=pl.ANY)] * (2 + len(tables)),
-        out_specs=pl.BlockSpec(memory_space=pl.ANY),
+        out_shape=pltpu.VMEM((2, PAIRS, LAGS, 2 * LAGS), F32),
+        in_specs=[pl.BlockSpec(memory_space=pltpu.HBM)] * (4 + len(tables)),
+        out_specs=vmem,
         scratch_shapes=[pltpu.VMEM(t.shape, t.dtype) for t in tables]
         + [
+            pltpu.SMEM((2,), jnp.int32),
+            pltpu.SMEM((2,), jnp.int32),
             pltpu.VMEM((ROWS + 2 * REF_HALO, COLS + 2 * LANE), F32),
             pltpu.VMEM((ROWS + 2 * ROW_HALO, COLS + 2 * LANE), F32),
             pltpu.VMEM((2, 2, 128, 3 * REACH), BF16),
             pltpu.VMEM((2, 64, 2 * REACH), BF16),
             pltpu.VMEM((2, 64, 2 * FAR), BF16),
-            pltpu.VMEM((2, ROWS + 2 * ROW_HALO, WIDE), BF16),
-            pltpu.VMEM((2, ROWS + 2 * ROW_HALO, WIDE), BF16),
-            pltpu.VMEM((2, ROWS + 2 * ROW_HALO, WIDE), BF16),
-            pltpu.VMEM((2, ROWS + 2 * ROW_HALO, WIDE), BF16),
+        ]
+        + [pltpu.VMEM((2, ROWS + 2 * ROW_HALO, WIDE), BF16)] * 4
+        + [
             pltpu.VMEM((3, BLOCKS, 64, 256), F32),
             pltpu.VMEM((2, 2, BLOCKS, 64, 256), F32),
+            pltpu.VMEM((2, BLOCKS - 1, 128, 128), F32),
             pltpu.VMEM((2, 128, WIDE), F32),
             pltpu.VMEM((8, WIDE), F32),
-            pltpu.VMEM((2 * CHIPS, 128, 128), F32),
-            pltpu.SemaphoreType.DMA,
             pltpu.SemaphoreType.DMA((2,)),
             pltpu.SemaphoreType.DMA((8,)),
             pltpu.SemaphoreType.DMA((48,)),
             pltpu.SemaphoreType.DMA((48,)),
         ],
-        compiler_params=pltpu.CompilerParams(collective_id=0, has_side_effects=True),
+        compiler_params=pltpu.CompilerParams(
+            collective_id=0, has_side_effects=True
+        ),
     )(off_az, off_rg, ref_image, sec_image, *[jnp.asarray(t) for t in tables])
+    out = pl.pallas_call(
+        oversample,
+        out_shape=jax.ShapeDtypeStruct((2 * CHIPS, 128, 128), F32),
+        in_specs=[vmem],
+        out_specs=anywhere,
+        scratch_shapes=[pltpu.VMEM((2 * CHIPS, 128, 128), F32), pltpu.SemaphoreType.DMA],
+        compiler_params=pltpu.CompilerParams(vmem_limit_bytes=8 << 20),
+    )(scores)
     return out.reshape(2, CHIPS, 128, 128)
 
 

time: 23 us -> 20 us (0.87)
  local copies, waits for them, and re-layouts: 2.7 us -> 0 us
    unnamed x1 -> x0, local copies, waits for them, and re-layouts: 2.7 us -> none
    pallas_call x1 -> x2, Pallas kernels: 20.1 us -> 19.9 us  [the longest x1 18.1 us: body(): pl.pallas_call(kernel, out_shape=pltpu.VMEM((2, PAIRS, LAGS, 2 * LAGS), F...]
where the time goes in v4:
time: 20 us; the launch traced here: 19.9 us
  Pallas kernels  19.9 us (99%)
    pallas_call x1, Pallas kernels, body(): pl.pallas_call(kernel, out_shape=pltpu.VMEM((2, PAIRS, LAGS, 2 * LAGS), F...  18.1 us
    pallas_call x1, Pallas kernels, body(): pl.pallas_call(oversample, out_shape=jax.ShapeDtypeStruct((2 * CHIPS, 128...  1.79 us

profile of v4, /device:TPU:99, one launch (start us, length us, event | category | flops | bytes accessed | tf_op | source)
XLA Modules:
  0.0 19.9 jit_solution(759987259322606067)
XLA Ops:
  0.0 18.1 %shard_map.100.score_ref = f32[2,6,64,128]{3,2,1,0:T(8,128)S(1)} custom-call(s32[2]{0:T(128)} %off_az_hbm.1, s32[2]{0:T(128)} %off_rg_hbm.1, f32[128,768]{1,0:T(8,128)} %ref_tile.1, f32[128,768]{1,0:T(8,128)} %sec_tile.1, bf16[3,128,192]{2,1,0:T(8,128)(2,1)} %constant.12.clone.refs_0_, f32[3,128,512]{2,1,0:T(8,128)} %constant.13.clone.refs_1_, ...), custom_call_target="tpu_custom_call" | custom-call | tf_op jit(solution)/shard_map/pallas_call | solution.py:536
  18.1 1.8 %shard_map.101 = f32[24,128,128]{2,1,0:T(8,128)} custom-call(f32[2,6,64,128]{3,2,1,0:T(8,128)S(1)} %shard_map.100.score_ref), custom_call_target="tpu_custom_call" | custom-call | tf_op jit(solution)/shard_map/pallas_call | solution.py:567

commit v5 on v4

--- a/solution.py
+++ b/solution.py
@@ -250,11 +250,11 @@
     everything = (LANE, COLS)
     near = halo.along_azimuth(sec_buf, ROW_HALO, 0, NEAR, everything)
     beside = halo.along_range(sec_buf, (ROW_HALO, ROWS)) + halo.along_range(ref_buf, (REF_HALO, ROWS))
-    order = (1, 6, 2, 5, 3, 4)
+    order = (1, 6, 2, 3, 4, 5)
     sec_far, ref_far = {}, {}
     for b in order:
-        sec_far[b] = halo.along_azimuth(sec_buf, ROW_HALO, NEAR, ROW_HALO, (LANE * b, LANE))
-    for b, lanes in ((1, (LANE, LANE)), (6, (COLS, LANE)), (2, (2 * LANE, 4 * LANE))):
+        lanes = (LANE * b, LANE)
+        sec_far[b] = halo.along_azimuth(sec_buf, ROW_HALO, NEAR, ROW_HALO, lanes)
         ref_far[b] = halo.along_azimuth(ref_buf, REF_HALO, 0, REF_HALO, lanes)
     near_corners = halo.corners(sec_buf, ROW_HALO, 0, NEAR)
     sec_corners = halo.corners(sec_buf, ROW_HALO, NEAR, ROW_HALO)
@@ -276,9 +276,9 @@
     halo.start(near)
     halo.start(beside)
     halo.start(sec_far[1] + sec_far[6])
-    halo.start(ref_far[1] + ref_far[6] + ref_far[2])
+    halo.start(ref_far[1] + ref_far[6])
     for b in order[2:]:
-        halo.start(sec_far[b])
+        halo.start(sec_far[b] + ref_far[b])
 
     own = pl.ds(LANE, COLS)
     ref_mean = jnp.mean(ref_buf[pl.ds(REF_HALO, ROWS), own], keepdims=True)
@@ -364,18 +364,15 @@
             store(windows.at[0, 1], pairs, got[0])
             store(windows.at[1, 0], pairs, got[1])
 
-    def outer_quadrants(*groups):
-        rows_out = [[reference_lines(m, pairs) for m in (0, 2)] for pairs in groups]
-        for pairs, x in zip(groups, rows_out):
-            got = range_spectra(x, col_ref)
-            store(quads.at[0], pairs, got[0])
-            store(quads.at[2], pairs, got[1])
-
-    def outer_windows(*groups):
+    def outer(*groups):
         for pairs in groups:
             take_lines(0, ((0, FAR),), pairs)
             take_lines(1, ((224, FAR),), pairs)
-        rows_out = [[window_transform(k, k, pairs) for k in range(2)] for pairs in groups]
+        rows_out = [
+            [window_transform(k, k, pairs) for k in range(2)]
+            + [reference_lines(m, pairs) for m in (0, 2)]
+            for pairs in groups
+        ]
         for pairs in groups:
             for k in range(2):
                 for p in pairs:
@@ -384,8 +381,10 @@
                     boxes[k, 64:, LANE * p : LANE * p + LANE] += sums[:, 128:]
         for pairs, x in zip(groups, rows_out):
             got = range_spectra(x, col_ref)
-            for k in range(2):
-                store(windows.at[k, k], pairs, got[k])
+            store(windows.at[0, 0], pairs, got[0])
+            store(windows.at[1, 1], pairs, got[1])
+            store(quads.at[0], pairs, got[2])
+            store(quads.at[2], pairs, got[3])
 
     def product(k, m, n):
         q = quads[k + m, n]
@@ -454,8 +453,10 @@
     for k in range(2):
         take_lines(k, near_lines, inside)
     middle_windows((1, 2), (3, 4), (5,))
-    halo.arrive(sec_far[1] + sec_far[6])
-    halo.start(sec_corners)
+    halo.arrive(sec_far[1])
+    halo.start(sec_corners[0::2])
+    halo.arrive(sec_far[6])
+    halo.start(sec_corners[1::2])
     halo.arrive(beside)
     middle_quadrants((0, 6))
     halo.arrive(ref_far[1] + ref_far[6])
@@ -465,18 +466,16 @@
         take_lines(k, near_lines + ((ROW_HALO, ROWS),), (0, 6))
     middle_windows((0, 6))
     middle_strips(*range(BLOCKS - 1))
-    halo.arrive(ref_far[2])
-    outer_quadrants((1, 2), (3, 4), (5,))
-    halo.arrive(ref_corners)
-    outer_quadrants((0, 6))
-    halo.arrive(sec_far[2] + sec_far[5] + sec_corners)
-    outer_windows((1, 5), (0, 6))
-    halo.arrive(sec_far[3])
-    outer_windows((2,))
-    finish(0, 1, 5)
-    halo.arrive(sec_far[4])
-    outer_windows((3, 4))
-    finish(2, 3, 4)
+    halo.arrive(sec_far[2] + ref_far[2])
+    halo.arrive(sec_far[3] + ref_far[3])
+    outer((1, 2))
+    halo.arrive(sec_far[4] + ref_far[4])
+    outer((3,))
+    finish(1, 2)
+    halo.arrive(sec_corners + ref_corners)
+    halo.arrive(sec_far[5] + ref_far[5])
+    outer((4, 5), (0, 6))
+    finish(0, 3, 4, 5)
     halo.close()
 
 

time: 20 us -> 18.5 us (0.925)
  Pallas kernels: 19.9 us -> 18.3 us
    pallas_call x1, Pallas kernels: 18.1 us -> 16.6 us  [body(): pl.pallas_call(kernel, out_shape=pltpu.VMEM((2, PAIRS, LAGS, 2 * LAGS), F...]
where the time goes in v5:
time: 18.5 us; the launch traced here: 18.3 us
  Pallas kernels  18.3 us (99%)
    pallas_call x1, Pallas kernels, body(): pl.pallas_call(kernel, out_shape=pltpu.VMEM((2, PAIRS, LAGS, 2 * LAGS), F...  16.6 us
    pallas_call x1, Pallas kernels, body(): pl.pallas_call(oversample, out_shape=jax.ShapeDtypeStruct((2 * CHIPS, 128...  1.79 us

profile of v5, /device:TPU:99, one launch (start us, length us, event | category | flops | bytes accessed | tf_op | source)
XLA Modules:
  0.0 18.3 jit_solution(6418526435093059868)
XLA Ops:
  0.0 16.6 %shard_map.100.score_ref = f32[2,6,64,128]{3,2,1,0:T(8,128)S(1)} custom-call(s32[2]{0:T(128)} %off_az_hbm.1, s32[2]{0:T(128)} %off_rg_hbm.1, f32[128,768]{1,0:T(8,128)} %ref_tile.1, f32[128,768]{1,0:T(8,128)} %sec_tile.1, bf16[3,128,192]{2,1,0:T(8,128)(2,1)} %constant.12.clone.refs_0_, f32[3,128,512]{2,1,0:T(8,128)} %constant.13.clone.refs_1_, ...), custom_call_target="tpu_custom_call" | custom-call | tf_op jit(solution)/shard_map/pallas_call | solution.py:535
  16.6 1.8 %shard_map.101 = f32[24,128,128]{2,1,0:T(8,128)} custom-call(f32[2,6,64,128]{3,2,1,0:T(8,128)S(1)} %shard_map.100.score_ref), custom_call_target="tpu_custom_call" | custom-call | tf_op jit(solution)/shard_map/pallas_call | solution.py:566

commit v6 on v5

--- a/solution.py
+++ b/solution.py
@@ -211,18 +211,18 @@
         )
 
     @staticmethod
-    def start(entries):
+    def start(entries, given=True):
         for transfer, sends, _ in entries:
 
-            @pl.when(sends)
+            @pl.when(sends & given)
             def _(transfer=transfer):
                 transfer.start()
 
     @staticmethod
-    def arrive(entries):
+    def arrive(entries, given=True):
         for transfer, _, comes in entries:
 
-            @pl.when(comes)
+            @pl.when(comes & given)
             def _(transfer=transfer):
                 transfer.wait_recv()
 
@@ -260,6 +260,14 @@
     sec_corners = halo.corners(sec_buf, ROW_HALO, NEAR, ROW_HALO)
     ref_corners = halo.corners(ref_buf, REF_HALO, 0, REF_HALO)
 
+    corners = sec_corners + ref_corners
+
+    def forward(step):
+        for given, edges in cores:
+            b = edges[step]
+            halo.arrive(sec_far[b] + ref_far[b], given)
+            halo.start(corners[0::2] if b == 1 else corners[1::2], given)
+
     halo.greet()
     fetches = [
         pltpu.make_async_copy(source, target, table_sems.at[i])
@@ -269,17 +277,20 @@
     ]
     for fetch in fetches:
         fetch.start()
-    halo.clear()
     for load in halo.loads:
         load.wait()
     halo.meet()
     halo.start(near)
     halo.start(beside)
-    halo.start(sec_far[1] + sec_far[6])
-    halo.start(ref_far[1] + ref_far[6])
+    second = lax.rem(lax.axis_index("rg"), 2) == 1
+    cores = ((jnp.logical_not(second), (1, 6)), (second, (6, 1)))
+    for given, edges in cores:
+        for b in edges:
+            halo.start(sec_far[b] + ref_far[b], given)
     for b in order[2:]:
         halo.start(sec_far[b] + ref_far[b])
 
+    halo.clear()
     own = pl.ds(LANE, COLS)
     ref_mean = jnp.mean(ref_buf[pl.ds(REF_HALO, ROWS), own], keepdims=True)
     sec_mean = jnp.mean(sec_buf[pl.ds(ROW_HALO, ROWS), own], keepdims=True)
@@ -364,27 +375,26 @@
             store(windows.at[0, 1], pairs, got[0])
             store(windows.at[1, 0], pairs, got[1])
 
-    def outer(*groups):
-        for pairs in groups:
+    def outer(for_windows, for_quadrants):
+        for pairs in for_windows:
             take_lines(0, ((0, FAR),), pairs)
             take_lines(1, ((224, FAR),), pairs)
-        rows_out = [
-            [window_transform(k, k, pairs) for k in range(2)]
-            + [reference_lines(m, pairs) for m in (0, 2)]
-            for pairs in groups
-        ]
-        for pairs in groups:
+        rows_out = {}
+        for pairs in for_windows:
+            rows_out[pairs] = [(windows.at[k, k], window_transform(k, k, pairs)) for k in range(2)]
+        for pairs in for_quadrants:
+            found = [(quads.at[m], reference_lines(m, pairs)) for m in (0, 2)]
+            rows_out[pairs] = rows_out.get(pairs, []) + found
+        for pairs in for_windows:
             for k in range(2):
                 for p in pairs:
                     sums = box_lines(k, 224 * k, FAR, p, box_far)
                     boxes[k, :64, LANE * p : LANE * p + LANE] += sums[:, :128]
                     boxes[k, 64:, LANE * p : LANE * p + LANE] += sums[:, 128:]
-        for pairs, x in zip(groups, rows_out):
-            got = range_spectra(x, col_ref)
-            store(windows.at[0, 0], pairs, got[0])
-            store(windows.at[1, 1], pairs, got[1])
-            store(quads.at[0], pairs, got[2])
-            store(quads.at[2], pairs, got[3])
+        for pairs, found in rows_out.items():
+            got = range_spectra([x for _, x in found], col_ref)
+            for (target, _), blocks in zip(found, got):
+                store(target, pairs, blocks)
 
     def product(k, m, n):
         q = quads[k + m, n]
@@ -402,7 +412,9 @@
     def strip(k, n):
         if (k, n) not in done:
             done[k, n] = True
-            strips[k, n] += product(k, k, n)
+            value = strips[k, n] + product(k, k, n)
+            strips[k, n] = value
+            return value
         return strips[k, n]
 
     def finish(*pairs):
@@ -421,23 +433,24 @@
             high, low = split(jnp.concatenate([left + middle_, middle_ + right], axis=1))
             y = dot(back_row_ref[:, :256], jnp.concatenate([high, low], axis=0))
             inner[k, s] = y + dot(back_row_ref[:, 256:], high)
-        for k, s in items:
-            y = inner[k, s]
-            corr = 0.0
-            for i in range(2):
-                lanes = slice(LANE * i, LANE * i + LANE)
-                high, low = split(jnp.concatenate([y[:64, lanes], y[64:, lanes]], axis=1))
-                wide = dot(high, back_col_ref[i])
-                corr = corr + (wide[:, :128] + wide[:, 128:]) + dot(low, back_col_ref[i, :, :128])
-            high, low = split(boxes[k, :, s * LANE : s * LANE + 256])
-            box = dot(high, box_col_ref[...]) + dot(low, box_col_ref[...])
-            first, second = box[:64], box[64:]
+        corr = 0.0
+        for i in range(2):
+            lanes = slice(LANE * i, LANE * i + LANE)
+            parts = [split(jnp.concatenate([inner[item][:64, lanes], inner[item][64:, lanes]], axis=1)) for item in items]
+            wide = dot(jnp.concatenate([high for high, _ in parts], axis=0), back_col_ref[i])
+            corr = corr + (wide[:, :128] + wide[:, 128:])
+            corr = corr + dot(jnp.concatenate([low for _, low in parts], axis=0), back_col_ref[i, :, :128])
+        parts = [split(boxes[k, :, s * LANE : s * LANE + 256]) for k, s in items]
+        box = dot(jnp.concatenate([high for high, _ in parts], axis=0), box_col_ref[...])
+        box = box + dot(jnp.concatenate([low for _, low in parts], axis=0), box_col_ref[...])
+        for i, (k, s) in enumerate(items):
+            first, second = box[128 * i : 128 * i + 64], box[128 * i + 64 : 128 * i + 128]
             both = moments[s]
             total = both[2 * k : 2 * k + 1] + both[2 * k + 2 : 2 * k + 3]
             power = both[2 * k + 1 : 2 * k + 2] + both[2 * k + 3 : 2 * k + 4]
             mean = total / AREA
             energy = power - total * mean
-            centered = corr - mean * first
+            centered = corr[64 * i : 64 * i + 64] - mean * first
             var_sum = jnp.maximum(second - first * first / AREA, 0.0)
             score_ref[k, s] = (CHIP / AREA) * centered * lax.rsqrt(
                 (energy / AREA) * (var_sum / AREA) + EPSILON
@@ -453,29 +466,23 @@
     for k in range(2):
         take_lines(k, near_lines, inside)
     middle_windows((1, 2), (3, 4), (5,))
-    halo.arrive(sec_far[1])
-    halo.start(sec_corners[0::2])
-    halo.arrive(sec_far[6])
-    halo.start(sec_corners[1::2])
+    forward(0)
     halo.arrive(beside)
     middle_quadrants((0, 6))
-    halo.arrive(ref_far[1] + ref_far[6])
-    halo.start(ref_corners)
+    forward(1)
     halo.arrive(near_corners)
     for k in range(2):
         take_lines(k, near_lines + ((ROW_HALO, ROWS),), (0, 6))
     middle_windows((0, 6))
     middle_strips(*range(BLOCKS - 1))
-    halo.arrive(sec_far[2] + ref_far[2])
-    halo.arrive(sec_far[3] + ref_far[3])
-    outer((1, 2))
+    halo.arrive(sec_far[2] + ref_far[2] + sec_far[3] + ref_far[3])
+    outer([(1, 2)], [(1, 2)])
     halo.arrive(sec_far[4] + ref_far[4])
-    outer((3,))
-    finish(1, 2)
-    halo.arrive(sec_corners + ref_corners)
+    outer([(3,)], [(3,)])
+    halo.arrive(corners)
     halo.arrive(sec_far[5] + ref_far[5])
-    outer((4, 5), (0, 6))
-    finish(0, 3, 4, 5)
+    outer([(4, 5), (0, 6)], [(4, 5), (0, 6)])
+    finish(0, 1, 2, 3, 4, 5)
     halo.close()
 
 
@@ -496,21 +503,23 @@
     right = jnp.concatenate(
         [jnp.where(row < LAGS, right, 0.0), jnp.where(row < LAGS, 0.0, right)], axis=1
     ).astype(BF16)
+    right = jnp.concatenate([right, right], axis=0)
     items = [(k, s) for k in range(2) for s in range(PAIRS)]
-    for some in (items[:4], items[4:8], items[8:]):
+    for first, last in ((0, 4), (4, 8), (8, 12)):
         lifted = []
-        for k, s in some:
-            high, low = split(score_ref[k, s])
-            lifted.append(dot(left, jnp.concatenate([high, low], axis=0)))
-        for (k, s), value in zip(some, lifted):
-            high, low = split(value)
-            wide = dot(high, right) + dot(low, right)
+        for i in range(first, last, 2):
+            parts = [split(score_ref[k, s]) for k, s in items[i : i + 2]]
+            high = jnp.concatenate([high for high, _ in parts], axis=1)
+            low = jnp.concatenate([low for _, low in parts], axis=1)
+            both = dot(left, jnp.concatenate([high, low], axis=0))
+            lifted += [both[:, :LANE], both[:, LANE:]]
+        for (k, s), value in zip(items[first:last], lifted):
+            wide = dot(jnp.concatenate(split(value), axis=1), right)
             at = k * CHIPS + 2 * s
             staged[at] = wide[:, :128]
             staged[at + 1] = wide[:, 128:]
-        for k, s in some:
-            part = pl.ds(k * CHIPS + 2 * s, 2)
-            pltpu.make_async_copy(staged.at[part], out_ref.at[part], sem).start()
+        part = pl.ds(2 * first, 2 * (last - first))
+        pltpu.make_async_copy(staged.at[part], out_ref.at[part], sem).start()
     pltpu.make_async_copy(staged, out_ref, sem).wait()
 
 

time: 18.5 us -> 18.1 us (0.978)
  Pallas kernels: 18.3 us -> 18 us
    pallas_call x1, Pallas kernels: 16.6 us -> 16.4 us  [body(): pl.pallas_call(kernel, out_shape=pltpu.VMEM((2, PAIRS, LAGS, 2 * LAGS), F...]
where the time goes in v6:
time: 18.1 us; the launch traced here: 18 us
  Pallas kernels  18 us (99%)
    pallas_call x1, Pallas kernels, body(): pl.pallas_call(kernel, out_shape=pltpu.VMEM((2, PAIRS, LAGS, 2 * LAGS), F...  16.4 us
    pallas_call x1, Pallas kernels, body(): pl.pallas_call(oversample, out_shape=jax.ShapeDtypeStruct((2 * CHIPS, 128...  1.6 us

profile of v6, /device:TPU:99, one launch (start us, length us, event | category | flops | bytes accessed | tf_op | source)
XLA Modules:
  0.0 18.0 jit_solution(3575933937171635822)
XLA Ops:
  0.0 16.4 %shard_map.100.score_ref = f32[2,6,64,128]{3,2,1,0:T(8,128)S(1)} custom-call(s32[2]{0:T(128)} %off_az_hbm.1, s32[2]{0:T(128)} %off_rg_hbm.1, f32[128,768]{1,0:T(8,128)} %ref_tile.1, f32[128,768]{1,0:T(8,128)} %sec_tile.1, bf16[3,128,192]{2,1,0:T(8,128)(2,1)} %constant.12.clone.refs_0_, f32[3,128,512]{2,1,0:T(8,128)} %constant.13.clone.refs_1_, ...), custom_call_target="tpu_custom_call" | custom-call | tf_op jit(solution)/shard_map/pallas_call | solution.py:544
  16.4 1.6 %shard_map.101 = f32[24,128,128]{2,1,0:T(8,128)} custom-call(f32[2,6,64,128]{3,2,1,0:T(8,128)S(1)} %shard_map.100.score_ref), custom_call_target="tpu_custom_call" | custom-call | tf_op jit(solution)/shard_map/pallas_call | solution.py:575

commit v7 on v6

--- a/solution.py
+++ b/solution.py
@@ -287,8 +287,9 @@
     for given, edges in cores:
         for b in edges:
             halo.start(sec_far[b] + ref_far[b], given)
+    late = (4, 5)
     for b in order[2:]:
-        halo.start(sec_far[b] + ref_far[b])
+        halo.start(sec_far[b] + ref_far[b], jnp.logical_not(second) if b in late else True)
 
     halo.clear()
     own = pl.ds(LANE, COLS)
@@ -466,15 +467,18 @@
     for k in range(2):
         take_lines(k, near_lines, inside)
     middle_windows((1, 2), (3, 4), (5,))
+    for b in late:
+        halo.start(sec_far[b] + ref_far[b], second)
     forward(0)
     halo.arrive(beside)
     middle_quadrants((0, 6))
+    middle_strips(*range(2, 11))
     forward(1)
     halo.arrive(near_corners)
     for k in range(2):
         take_lines(k, near_lines + ((ROW_HALO, ROWS),), (0, 6))
     middle_windows((0, 6))
-    middle_strips(*range(BLOCKS - 1))
+    middle_strips(0, 1, 11, 12)
     halo.arrive(sec_far[2] + ref_far[2] + sec_far[3] + ref_far[3])
     outer([(1, 2)], [(1, 2)])
     halo.arrive(sec_far[4] + ref_far[4])

time: 18.1 us -> 18.1 us (level)
  no operation moved by 1% of the time
where the time goes in v7:
time: 18.1 us; the launch traced here: 17.9 us
  Pallas kernels  17.9 us (99%)
    pallas_call x1, Pallas kernels, body(): pl.pallas_call(kernel, out_shape=pltpu.VMEM((2, PAIRS, LAGS, 2 * LAGS), F...  16.3 us
    pallas_call x1, Pallas kernels, body(): pl.pallas_call(oversample, out_shape=jax.ShapeDtypeStruct((2 * CHIPS, 128...  1.6 us

profile of v7, /device:TPU:99, one launch (start us, length us, event | category | flops | bytes accessed | tf_op | source)
XLA Modules:
  0.0 17.9 jit_solution(7469836115213350931)
XLA Ops:
  0.0 16.3 %shard_map.100.score_ref = f32[2,6,64,128]{3,2,1,0:T(8,128)S(1)} custom-call(s32[2]{0:T(128)} %off_az_hbm.1, s32[2]{0:T(128)} %off_rg_hbm.1, f32[128,768]{1,0:T(8,128)} %ref_tile.1, f32[128,768]{1,0:T(8,128)} %sec_tile.1, bf16[3,128,192]{2,1,0:T(8,128)(2,1)} %constant.12.clone.refs_0_, f32[3,128,512]{2,1,0:T(8,128)} %constant.13.clone.refs_1_, ...), custom_call_target="tpu_custom_call" | custom-call | tf_op jit(solution)/shard_map/pallas_call | solution.py:548
  16.3 1.6 %shard_map.101 = f32[24,128,128]{2,1,0:T(8,128)} custom-call(f32[2,6,64,128]{3,2,1,0:T(8,128)S(1)} %shard_map.100.score_ref), custom_call_target="tpu_custom_call" | custom-call | tf_op jit(solution)/shard_map/pallas_call | solution.py:579

commit v8 on v6

--- a/solution.py
+++ b/solution.py
@@ -469,12 +469,13 @@
     forward(0)
     halo.arrive(beside)
     middle_quadrants((0, 6))
+    middle_strips(*range(2, 11))
     forward(1)
     halo.arrive(near_corners)
     for k in range(2):
         take_lines(k, near_lines + ((ROW_HALO, ROWS),), (0, 6))
     middle_windows((0, 6))
-    middle_strips(*range(BLOCKS - 1))
+    middle_strips(0, 1, 11, 12)
     halo.arrive(sec_far[2] + ref_far[2] + sec_far[3] + ref_far[3])
     outer([(1, 2)], [(1, 2)])
     halo.arrive(sec_far[4] + ref_far[4])
@@ -505,7 +506,7 @@
     ).astype(BF16)
     right = jnp.concatenate([right, right], axis=0)
     items = [(k, s) for k in range(2) for s in range(PAIRS)]
-    for first, last in ((0, 4), (4, 8), (8, 12)):
+    for first, last in ((0, 6), (6, 12)):
         lifted = []
         for i in range(first, last, 2):
             parts = [split(score_ref[k, s]) for k, s in items[i : i + 2]]

time: 18.1 us -> 18.1 us (level)
  no operation moved by 1% of the time
where the time goes in v8:
time: 18.1 us; the launch traced here: 17.9 us
  Pallas kernels  17.9 us (99%)
    pallas_call x1, Pallas kernels, body(): pl.pallas_call(kernel, out_shape=pltpu.VMEM((2, PAIRS, LAGS, 2 * LAGS), F...  16.3 us
    pallas_call x1, Pallas kernels, body(): pl.pallas_call(oversample, out_shape=jax.ShapeDtypeStruct((2 * CHIPS, 128...  1.56 us

profile of v8, /device:TPU:99, one launch (start us, length us, event | category | flops | bytes accessed | tf_op | source)
XLA Modules:
  0.0 17.9 jit_solution(2651931527383023845)
XLA Ops:
  0.0 16.3 %shard_map.100.score_ref = f32[2,6,64,128]{3,2,1,0:T(8,128)S(1)} custom-call(s32[2]{0:T(128)} %off_az_hbm.1, s32[2]{0:T(128)} %off_rg_hbm.1, f32[128,768]{1,0:T(8,128)} %ref_tile.1, f32[128,768]{1,0:T(8,128)} %sec_tile.1, bf16[3,128,192]{2,1,0:T(8,128)(2,1)} %constant.12.clone.refs_0_, f32[3,128,512]{2,1,0:T(8,128)} %constant.13.clone.refs_1_, ...), custom_call_target="tpu_custom_call" | custom-call | tf_op jit(solution)/shard_map/pallas_call | solution.py:545
  16.3 1.6 %shard_map.101 = f32[24,128,128]{2,1,0:T(8,128)} custom-call(f32[2,6,64,128]{3,2,1,0:T(8,128)S(1)} %shard_map.100.score_ref), custom_call_target="tpu_custom_call" | custom-call | tf_op jit(solution)/shard_map/pallas_call | solution.py:576

commit v9 on v8

--- a/solution.py
+++ b/solution.py
@@ -129,10 +129,11 @@
     def __init__(self, tiles, bufs, tile_sems, send_sems, recv_sems):
         az, rg = lax.axis_index("az"), lax.axis_index("rg")
         last_az, last_rg = lax.axis_size("az") - 1, lax.axis_size("rg") - 1
-        self.up = ("az", az - 1, az > 0)
-        self.down = ("az", az + 1, az < last_az)
-        self.left = ("rg", rg - 1, rg > 0)
-        self.right = ("rg", rg + 1, rg < last_rg)
+        self.place = {"az": az, "rg": rg}
+        self.up = ("az", -1, az > 0)
+        self.down = ("az", 1, az < last_az)
+        self.left = ("rg", -1, rg > 0)
+        self.right = ("rg", 1, rg < last_rg)
         self.sides = (self.up, self.down, self.left, self.right)
         self.bufs, self.send_sems, self.recv_sems, self.count = bufs, send_sems, recv_sems, 0
         self.all = []
@@ -145,11 +146,12 @@
         for load in self.loads:
             load.start()
         barrier = pltpu.get_barrier_semaphore()
-        for axis, place, there in self.sides:
+        for axis, step, there in self.sides:
 
             @pl.when(there)
-            def _(axis=axis, place=place):
-                pl.semaphore_signal(barrier, inc=1, device_id={axis: place}, device_id_type=MESH)
+            def _(axis=axis, step=step):
+                peer = {axis: self.place[axis] + step}
+                pl.semaphore_signal(barrier, inc=1, device_id=peer, device_id_type=MESH)
 
     def clear(self):
         up, down, left, right = self.sides
@@ -174,21 +176,21 @@
     def copy(self, buf, rows, lanes, to_rows, to_lanes, side, back, have=None):
         index = self.count
         self.count += 1
-        axis, place, sends = side
-        comes = back[2]
+        axis, step, sends = side
+        comes, name = back[2], None
         if have is not None:
-            sends, comes = sends & have, comes & have
+            name = have[1]
+            sends, comes = sends & have[2], comes & have[2]
         transfer = pltpu.make_async_remote_copy(
             src_ref=buf.at[pl.ds(*rows), pl.ds(*lanes)],
             dst_ref=buf.at[pl.ds(*to_rows), pl.ds(*to_lanes)],
             send_sem=self.send_sems.at[index],
             recv_sem=self.recv_sems.at[index],
-            device_id={axis: place},
+            device_id={axis: self.place[axis] + step},
             device_id_type=MESH,
         )
-        entry = (transfer, sends, comes)
-        self.all.append(entry)
-        return entry
+        self.all.append((transfer, sends, comes, (axis, step, name), (axis, -step, name)))
+        return self.all[-1]
 
     def along_azimuth(self, buf, halo, near, far, lanes):
         count = far - near
@@ -206,32 +208,30 @@
 
     def corners(self, buf, halo, near, far):
         count = far - near
-        return self.along_range(buf, (halo - far, count), self.up[2]) + self.along_range(
-            buf, (halo + ROWS + near, count), self.down[2]
+        return self.along_range(buf, (halo - far, count), self.up) + self.along_range(
+            buf, (halo + ROWS + near, count), self.down
         )
 
     @staticmethod
-    def start(entries, given=True):
-        for transfer, sends, _ in entries:
-
-            @pl.when(sends & given)
-            def _(transfer=transfer):
-                transfer.start()
-
-    @staticmethod
-    def arrive(entries, given=True):
-        for transfer, _, comes in entries:
-
-            @pl.when(comes & given)
-            def _(transfer=transfer):
-                transfer.wait_recv()
+    def each(entries, act, coming, given=True):
+        together = {}
+        for entry in entries:
+            together.setdefault(entry[4 if coming else 3], []).append(entry)
+        for some in together.values():
+
+            @pl.when(some[0][2 if coming else 1] & given)
+            def _(some=some):
+                for entry in some:
+                    act(entry[0])
+
+    def start(self, entries, given=True):
+        self.each(entries, lambda transfer: transfer.start(), False, given)
+
+    def arrive(self, entries, given=True):
+        self.each(entries, lambda transfer: transfer.wait_recv(), True, given)
 
     def close(self):
-        for transfer, sends, _ in self.all:
-
-            @pl.when(sends)
-            def _(transfer=transfer):
-                transfer.wait_send()
+        self.each(self.all, lambda transfer: transfer.wait_send(), False)
 
 
 def kernel(off_az_hbm, off_rg_hbm, ref_tile, sec_tile, *refs):
@@ -260,6 +260,8 @@
     sec_corners = halo.corners(sec_buf, ROW_HALO, NEAR, ROW_HALO)
     ref_corners = halo.corners(ref_buf, REF_HALO, 0, REF_HALO)
 
+    second = lax.rem(lax.axis_index("rg"), 2) == 1
+    cores = ((jnp.logical_not(second), (1, 6)), (second, (6, 1)))
     corners = sec_corners + ref_corners
 
     def forward(step):
@@ -280,15 +282,11 @@
     for load in halo.loads:
         load.wait()
     halo.meet()
-    halo.start(near)
     halo.start(beside)
-    second = lax.rem(lax.axis_index("rg"), 2) == 1
-    cores = ((jnp.logical_not(second), (1, 6)), (second, (6, 1)))
-    for given, edges in cores:
-        for b in edges:
-            halo.start(sec_far[b] + ref_far[b], given)
-    for b in order[2:]:
-        halo.start(sec_far[b] + ref_far[b])
+    rest = [entry for b in order[2:] for entry in sec_far[b] + ref_far[b]]
+    for given, (b, c) in cores:
+        edges = sec_far[b] + ref_far[b] + sec_far[c] + ref_far[c]
+        halo.start(near + edges + rest, given)
 
     halo.clear()
     own = pl.ds(LANE, COLS)

time: 18.1 us -> 18.1 us (level)
  no operation moved by 1% of the time
where the time goes in v9:
time: 18.1 us; the launch traced here: 17.9 us
  Pallas kernels  17.9 us (99%)
    pallas_call x1, Pallas kernels, body(): pl.pallas_call(kernel, out_shape=pltpu.VMEM((2, PAIRS, LAGS, 2 * LAGS), F...  16.3 us
    pallas_call x1, Pallas kernels, body(): pl.pallas_call(oversample, out_shape=jax.ShapeDtypeStruct((2 * CHIPS, 128...  1.56 us

profile of v9, /device:TPU:99, one launch (start us, length us, event | category | flops | bytes accessed | tf_op | source)
XLA Modules:
  0.0 17.9 jit_solution(7565437459654055274)
XLA Ops:
  0.0 16.3 %shard_map.100.score_ref = f32[2,6,64,128]{3,2,1,0:T(8,128)S(1)} custom-call(s32[2]{0:T(128)} %off_az_hbm.1, s32[2]{0:T(128)} %off_rg_hbm.1, f32[128,768]{1,0:T(8,128)} %ref_tile.1, f32[128,768]{1,0:T(8,128)} %sec_tile.1, bf16[3,128,192]{2,1,0:T(8,128)(2,1)} %constant.12.clone.refs_0_, f32[3,128,512]{2,1,0:T(8,128)} %constant.13.clone.refs_1_, ...), custom_call_target="tpu_custom_call" | custom-call | tf_op jit(solution)/shard_map/pallas_call | solution.py:543
  16.4 1.6 %shard_map.101 = f32[24,128,128]{2,1,0:T(8,128)} custom-call(f32[2,6,64,128]{3,2,1,0:T(8,128)S(1)} %shard_map.100.score_ref), custom_call_target="tpu_custom_call" | custom-call | tf_op jit(solution)/shard_map/pallas_call | solution.py:574

commit v10 on v8

--- a/solution.py
+++ b/solution.py
@@ -506,7 +506,7 @@
     ).astype(BF16)
     right = jnp.concatenate([right, right], axis=0)
     items = [(k, s) for k in range(2) for s in range(PAIRS)]
-    for first, last in ((0, 6), (6, 12)):
+    for first, last in ((0, 4), (4, 12)):
         lifted = []
         for i in range(first, last, 2):
             parts = [split(score_ref[k, s]) for k, s in items[i : i + 2]]

time: 18.1 us -> 18.2 us (level)
  no operation moved by 1% of the time
where the time goes in v10:
time: 18.2 us; the launch traced here: 18 us
  Pallas kernels  18 us (99%)
    pallas_call x1, Pallas kernels, body(): pl.pallas_call(kernel, out_shape=pltpu.VMEM((2, PAIRS, LAGS, 2 * LAGS), F...  16.3 us
    pallas_call x1, Pallas kernels, body(): pl.pallas_call(oversample, out_shape=jax.ShapeDtypeStruct((2 * CHIPS, 128...  1.64 us

profile of v10, /device:TPU:99, one launch (start us, length us, event | category | flops | bytes accessed | tf_op | source)
XLA Modules:
  0.0 18.0 jit_solution(15331273507963697966)
XLA Ops:
  0.0 16.3 %shard_map.100.score_ref = f32[2,6,64,128]{3,2,1,0:T(8,128)S(1)} custom-call(s32[2]{0:T(128)} %off_az_hbm.1, s32[2]{0:T(128)} %off_rg_hbm.1, f32[128,768]{1,0:T(8,128)} %ref_tile.1, f32[128,768]{1,0:T(8,128)} %sec_tile.1, bf16[3,128,192]{2,1,0:T(8,128)(2,1)} %constant.12.clone.refs_0_, f32[3,128,512]{2,1,0:T(8,128)} %constant.13.clone.refs_1_, ...), custom_call_target="tpu_custom_call" | custom-call | tf_op jit(solution)/shard_map/pallas_call | solution.py:545
  16.3 1.6 %shard_map.101 = f32[24,128,128]{2,1,0:T(8,128)} custom-call(f32[2,6,64,128]{3,2,1,0:T(8,128)S(1)} %shard_map.100.score_ref), custom_call_target="tpu_custom_call" | custom-call | tf_op jit(solution)/shard_map/pallas_call | solution.py:576
